TPU v7x, 8 devices: a whole 2x2x1 slice. The times are simulated.
8 devices in a mesh: part: 1 (over z), row: 2 (over y), col: 4 (over x, core).
Axes of the slice: x: 2, y: 2, z: 1, core: 2. Of those that a mesh axis runs over, the one named last changes fastest.
Arguments:
- counts: bfloat16 [2048, 65536], P(('part', 'row'), 'col')
- w_init: float32 [2048, 256], P(('part', 'row'))
- h_init: float32 [256, 65536], P('part', 'col')
Outputs:
- output 1: float32 [2048, 256], P(('part', 'row'))
- output 2: float32 [256, 65536], P('part', 'col')
All inputs are finite; a program needn't handle non-finite values.
Results may differ from a plain program's by a relative error of at most 0.001.
Values are sent between devices in bfloat16 or wider.
A program may use at most 1 GiB of HBM per device.

v0:
```python
import jax
import jax.numpy as jnp
from jax import lax
from jax.sharding import PartitionSpec as P

SWEEPS = 6


def solution(mesh):
    def local_sweeps(count_blk, w_blk, h_blk):
        w_state = w_blk
        h_state = h_blk
        for sweep_idx in range(SWEEPS):
            w_bf = w_state.astype(jnp.bfloat16)
            h_bf = h_state.astype(jnp.bfloat16)
            z_local = jnp.dot(w_bf, h_bf, preferred_element_type=jnp.float32)
            q_local = (count_blk.astype(jnp.float32) / z_local).astype(jnp.bfloat16)
            num_w = lax.dot_general(q_local, h_bf, (((1,), (1,)), ((), ())), preferred_element_type=jnp.float32)
            num_h = lax.dot_general(w_bf, q_local, (((0,), (0,)), ((), ())), preferred_element_type=jnp.float32)
            h_rowsum = jnp.sum(h_state, axis=1)
            w_colsum = jnp.sum(w_state, axis=0)
            num_w = lax.psum(num_w, "col")
            h_rowsum = lax.psum(h_rowsum, "col")
            num_h = lax.psum(num_h, "row")
            w_colsum = lax.psum(w_colsum, "row")
            w_state = w_state * num_w / h_rowsum[None, :]
            h_state = h_state * num_h / w_colsum[:, None]
        return w_state, h_state

    return jax.shard_map(
        local_sweeps,
        mesh=mesh,
        in_specs=(P(("part", "row"), "col"), P(("part", "row"), None), P("part", "col")),
        out_specs=(P(("part", "row"), None), P("part", "col")),
        check_vma=False,
    )
```

profile of v0, /device:TPU:0, one launch (start us, length us, event | category | flops | bytes accessed | tf_op | source)
XLA Modules:
  0.0 2845.0 jit_solution(3568789925867421168)
XLA Ops:
  7.2 30.9 %fusion = bf16[1024,16384]{1,0:T(8,128)(2,1)} fusion(bf16[1024,16384]{1,0:T(8,128)(2,1)} %param.3, f32[256,16384]{1,0:T(8,128)} %param.5, f32[1024,256]{1,0:T(8,128)} %param.4), kind=kOutput, calls=%fused_computation.6 | convolution fusion | flops 8644722688 | bytes 84934656 | tf_op jit(solution)/shard_map/dot_general | solution.py:16
  38.1 18.6 convolution_bitcast_fusion
  56.8 20.4 fusion.21
  77.7 6.7 reduce_sum.108
  84.4 17.4 copy.5
  101.8 6.4 psum.171
  108.2 323.8 %all-reduce.20.cloned.1.call-done = f32[256,16384]{0,1:T(8,128)} async-done(((f32[256,16384]{0,1:T(8,128)}), f32[256,16384]{0,1:T(8,128)}) %all-reduce.20.cloned.1.call-update) | async-done | bytes 16777232 | tf_op jit(solution)/shard_map/psum | solution.py:24
  432.0 17.6 fusion.50
  449.6 6.3 all-reduce.2
  455.9 10.2 all-reduce.18.cloned.1.call-done
  466.1 1.4 fusion.49
  467.6 31.2 %fusion.1 = bf16[1024,16384]{1,0:T(8,128)(2,1)} fusion(bf16[1024,16384]{1,0:T(8,128)(2,1)} %param.3, f32[256,16384]{0,1:T(8,128)} %get-tuple-element.33, f32[1024,256]{1,0:T(8,128)S(1)} %get-tuple-element.31), kind=kOutput, calls=%fused_computation.7 | convolution fusion | flops 8644722688 | bytes 84934656 | tf_op jit(solution)/shard_map/dot_general | solution.py:16
  498.8 20.8 fusion.18
  519.7 23.3 fusion.36
  543.1 7.8 all-reduce.22.cloned.1.call-done
  552.3 13.7 all-reduce.4
  566.0 359.7 %all-reduce.24.cloned.1.call-done = f32[256,16384]{0,1:T(8,128)} async-done(((f32[256,16384]{0,1:T(8,128)}), f32[256,16384]{0,1:T(8,128)}) %all-reduce.24.cloned.1.call-update) | async-done | bytes 16777232 | tf_op jit(solution)/shard_map/psum | solution.py:24
  925.7 17.6 fusion.47
  943.3 31.2 %fusion.2 = bf16[1024,16384]{1,0:T(8,128)(2,1)} fusion(bf16[1024,16384]{1,0:T(8,128)(2,1)} %param.3, f32[256,16384]{0,1:T(8,128)} %get-tuple-element.27, f32[1024,256]{1,0:T(8,128)S(1)} %get-tuple-element.29), kind=kOutput, calls=%fused_computation.8 | convolution fusion | flops 8644722688 | bytes 84934656 | tf_op jit(solution)/shard_map/dot_general | solution.py:16
  974.5 23.3 fusion.33
  997.9 20.8 fusion.15
  1019.2 351.3 %all-reduce.28.cloned.1.call-done = f32[256,16384]{0,1:T(8,128)} async-done(((f32[256,16384]{0,1:T(8,128)}), f32[256,16384]{0,1:T(8,128)}) %all-reduce.28.cloned.1.call-update) | async-done | bytes 16777232 | tf_op jit(solution)/shard_map/psum | solution.py:24
  1370.5 17.6 fusion.46
  1388.1 6.3 all-reduce.1
  1394.4 10.1 all-reduce.26.cloned.1.call-done
  1405.9 31.2 %fusion.3 = bf16[1024,16384]{1,0:T(8,128)(2,1)} fusion(bf16[1024,16384]{1,0:T(8,128)(2,1)} %param.3, f32[256,16384]{0,1:T(8,128)} %get-tuple-element.25, f32[1024,256]{1,0:T(8,128)S(1)} %get-tuple-element.23), kind=kOutput, calls=%fused_computation.9 | convolution fusion | flops 8644722688 | bytes 84934656 | tf_op jit(solution)/shard_map/dot_general | solution.py:16
  1437.2 20.8 fusion.12
  1458.0 23.3 fusion.30
  1481.5 7.8 all-reduce.30.cloned.1.call-done
  1490.6 5.1 all-reduce.3
  1495.7 368.4 %all-reduce.32.cloned.1.call-done = f32[256,16384]{0,1:T(8,128)} async-done(((f32[256,16384]{0,1:T(8,128)}), f32[256,16384]{0,1:T(8,128)}) %all-reduce.32.cloned.1.call-update) | async-done | bytes 16777232 | tf_op jit(solution)/shard_map/psum | solution.py:24
  1864.1 17.6 fusion.43
  1881.7 31.2 %fusion.4 = bf16[1024,16384]{1,0:T(8,128)(2,1)} fusion(bf16[1024,16384]{1,0:T(8,128)(2,1)} %param.3, f32[256,16384]{0,1:T(8,128)} %get-tuple-element.19, f32[1024,256]{1,0:T(8,128)S(1)} %get-tuple-element.21), kind=kOutput, calls=%fused_computation.10 | convolution fusion | flops 8644722688 | bytes 84934656 | tf_op jit(solution)/shard_map/dot_general | solution.py:16
  1913.0 23.3 fusion.27
  1936.4 20.8 fusion.9
  1957.4 351.5 %all-reduce.36.cloned.1.call-done = f32[256,16384]{0,1:T(8,128)} async-done(((f32[256,16384]{0,1:T(8,128)}), f32[256,16384]{0,1:T(8,128)}) %all-reduce.36.cloned.1.call-update) | async-done | bytes 16777232 | tf_op jit(solution)/shard_map/psum | solution.py:24
  2309.0 17.6 fusion.42
  2326.6 6.3 all-reduce
  2332.8 10.1 all-reduce.34.cloned.1.call-done
  2344.4 31.2 %fusion.5 = bf16[1024,16384]{1,0:T(8,128)(2,1)} fusion(bf16[1024,16384]{1,0:T(8,128)(2,1)} %param.3, f32[256,16384]{0,1:T(8,128)} %get-tuple-element.17, f32[1024,256]{1,0:T(8,128)S(1)} %get-tuple-element.15), kind=kOutput, calls=%fused_computation.11 | convolution fusion | flops 8644722688 | bytes 84934656 | tf_op jit(solution)/shard_map/dot_general | solution.py:16
  2375.6 20.8 fusion.6
  2396.7 23.3 fusion.24
  2420.1 4.9 psum.191
  2425.0 2.7 all-reduce.38.cloned.1.call-done
  2427.7 2.3 multiply_divide_fusion.6
  2430.0 372.4 %all-reduce.40.cloned.1.call-done = f32[256,16384]{0,1:T(8,128)} async-done(((f32[256,16384]{0,1:T(8,128)}), f32[256,16384]{0,1:T(8,128)}) %all-reduce.40.cloned.1.call-update) | async-done | bytes 16777232 | tf_op jit(solution)/shard_map/psum | solution.py:24
  2802.4 17.9 multiply_divide_fusion
  2820.3 17.4 copy.11
  (31 shorter events, 7.7 us)
Async XLA Ops:
  7.2 31.0 %copy-start = (f32[1024,256]{1,0:T(8,128)S(1)}, f32[1024,256]{1,0:T(8,128)}, u32[]{:S(2)}) copy-start(f32[1024,256]{1,0:T(8,128)} %param.4) | copy-start | bytes 3145732
  7.2 424.8 %all-reduce.20.cloned.1.call-start = ((), (), s32[]{:S(2)}) async-start(), calls=%async_computation.1 | async-start | bytes 33554432 | tf_op jit(solution)/shard_map/psum | solution.py:24
  56.8 409.4 %all-reduce.18.cloned.1.call-start = ((), (), s32[]{:S(2)}) async-start(), calls=%async_computation | async-start | bytes 2097152 | tf_op jit(solution)/shard_map/psum | solution.py:22
  77.2 473.6 %all-reduce.22.cloned.1.call-start = ((), (), s32[]{:S(2)}) async-start(), calls=%async_computation.2 | async-start | bytes 2097152 | tf_op jit(solution)/shard_map/psum | solution.py:22
  519.6 406.1 %all-reduce.24.cloned.1.call-start = ((), (), s32[]{:S(2)}) async-start(), calls=%async_computation.3 | async-start | bytes 33554432 | tf_op jit(solution)/shard_map/psum | solution.py:24
  543.0 827.5 %all-reduce.28.cloned.1.call-start = ((), (), s32[]{:S(2)}) async-start(), calls=%async_computation.5 | async-start | bytes 33554432 | tf_op jit(solution)/shard_map/psum | solution.py:24
  997.9 406.6 %all-reduce.26.cloned.1.call-start = ((), (), s32[]{:S(2)}) async-start(), calls=%async_computation.4 | async-start | bytes 2097152 | tf_op jit(solution)/shard_map/psum | solution.py:22
  1018.8 470.5 %all-reduce.30.cloned.1.call-start = ((), (), s32[]{:S(2)}) async-start(), calls=%async_computation.6 | async-start | bytes 2097152 | tf_op jit(solution)/shard_map/psum | solution.py:22
  1458.0 406.1 %all-reduce.32.cloned.1.call-start = ((), (), s32[]{:S(2)}) async-start(), calls=%async_computation.7 | async-start | bytes 33554432 | tf_op jit(solution)/shard_map/psum | solution.py:24
  1481.4 827.5 %all-reduce.36.cloned.1.call-start = ((), (), s32[]{:S(2)}) async-start(), calls=%async_computation.9 | async-start | bytes 33554432 | tf_op jit(solution)/shard_map/psum | solution.py:24
  1936.3 406.6 %all-reduce.34.cloned.1.call-start = ((), (), s32[]{:S(2)}) async-start(), calls=%async_computation.8 | async-start | bytes 2097152 | tf_op jit(solution)/shard_map/psum | solution.py:22
  1957.2 470.5 %all-reduce.38.cloned.1.call-start = ((), (), s32[]{:S(2)}) async-start(), calls=%async_computation.10 | async-start | bytes 2097152 | tf_op jit(solution)/shard_map/psum | solution.py:22
  2396.4 406.0 %all-reduce.40.cloned.1.call-start = ((), (), s32[]{:S(2)}) async-start(), calls=%async_computation.11 | async-start | bytes 33554432 | tf_op jit(solution)/shard_map/psum | solution.py:24
Sparse Core Ops, SparseCore 0:
  56.9 375.0 all-reduce.19
  434.9 31.1 all-reduce.17
  519.7 31.0 all-reduce.21
  553.2 372.4 all-reduce.23
  998.0 372.4 all-reduce.27
  1373.3 31.1 all-reduce.25
  1458.1 31.0 all-reduce.29
  1491.7 372.4 all-reduce.31
  1936.4 372.4 all-reduce.35
  2311.7 31.1 all-reduce.33
  2396.5 31.0 all-reduce.37
  2430.0 372.3 all-reduce.39
where the time goes:
time: 2850 us; the launch traced here: 2840 us
  waiting for transfers between devices  2180 us (76%)
  matrix products  447 us (16%)
  other arithmetic  122 us (4%)
  blocking collectives  48.9 us (2%)
  local copies, waits for them, and re-layouts  34.9 us (1%)
    psum x6, waiting for transfers between devices, local_sweeps(): num_h = lax.psum(num_h, 'row')  2130 us
    dot_general x6, matrix products, local_sweeps(): z_local = jnp.dot(w_bf, h_bf, preferred_element_type=jnp.float32)  187 us
    dot_general x6, matrix products, local_sweeps(): lax.dot_general(w_bf, q_local, (((0,), (0,)), ((), ())), preferred_elemen...  135 us
    dot_general x6, matrix products, local_sweeps(): lax.dot_general(q_local, h_bf, (((1,), (1,)), ((), ())), preferred_elemen...  124 us
    reduce_sum x6, other arithmetic, local_sweeps(): h_rowsum = jnp.sum(h_state, axis=1)  94.7 us
  transfers between devices with their start and end apart: 12, of which 12 were waited for; matrix products, arithmetic and copies ran while one was open for 8% of the time, Pallas kernels for 0%

commit v1 on v0

v1 whole, which is shorter than its diff:
```python
import functools

import jax
import jax.numpy as jnp
from jax import lax
from jax.experimental import pallas as pl
from jax.experimental.pallas import tpu as pltpu
from jax.sharding import PartitionSpec as P

SWEEPS = 6
F32 = jnp.float32
BF16 = jnp.bfloat16
BV = 1024
VMEM = 60 * 1024 * 1024


def dot(a, b):
    return jnp.dot(a, b, preferred_element_type=F32)


def dot_t(a, b):
    return lax.dot_general(a, b, (((1,), (1,)), ((), ())), preferred_element_type=F32)


def ratio(c, z):
    return (c.astype(F32) / z).astype(BF16)


def lane_sum(h):
    out = h[:, :128]
    for g in range(1, h.shape[1] // 128):
        out = out + h[:, g * 128:(g + 1) * 128]
    return out


def first_kernel(row_ref, c_ref, wb_ref, wbt_ref, h_ref, nw_ref, nh_ref, hs_ref):
    j = pl.program_id(0)
    half = pl.num_programs(0) // 2

    @pl.when(j == 0)
    def _():
        nw_ref[...] = jnp.zeros_like(nw_ref)
        hs_ref[...] = jnp.zeros_like(hs_ref)

    hb = h_ref[...].astype(BF16)
    q = ratio(c_ref[...], dot(wb_ref[...], hb))
    nw_ref[...] += dot_t(q, hb)
    hs_ref[...] += lane_sum(h_ref[...])

    @pl.when(j < half)
    def _():
        nh_ref[...] = dot(wbt_ref[...], q)


def sweep_body(c_own, c_par, wb_ref, wbt_ref, ws, h, own, par, nw_ref, hs_ref):
    hb = h.astype(BF16)
    q_own = ratio(c_own[...], dot(wb_ref[own], hb))
    nw_ref[own] += dot_t(q_own, hb)
    nh = dot(wbt_ref[own], q_own)
    q_par = ratio(c_par[...], dot(wb_ref[par], hb))
    nw_ref[par] += dot_t(q_par, hb)
    nh = nh + dot(wbt_ref[par], q_par)
    new = h * nh / ws
    hs_ref[...] += lane_sum(new)
    return new


def chunk_kernel(row_ref, c_own, c_par, wb0_ref, wbt0_ref, ws0_ref, wb1_ref, wbt1_ref, ws1_ref, h_ref, nh_ref,
                 nw_in, hs1_in, hs2_in, h_out, nw_ref, hs1_ref, hs2_ref):
    own = row_ref[0]
    par = 1 - own
    nw_ref[...] = nw_in[...]
    hs1_ref[...] = hs1_in[...]
    hs2_ref[...] = hs2_in[...]
    h = h_ref[...]
    hb = h.astype(BF16)
    q = ratio(c_par[...], dot(wb0_ref[par], hb))
    nh = nh_ref[...] + dot(wbt0_ref[par], q)
    h = h * nh / ws0_ref[...]
    hs1_ref[...] += lane_sum(h)
    h_out[...] = sweep_body(c_own, c_par, wb1_ref, wbt1_ref, ws1_ref[...], h, own, par, nw_ref, hs2_ref)


def sweep_kernel(row_ref, c_own, c_par, wb_ref, wbt_ref, ws_ref, h_ref, h_out, nw_ref, hs_ref):
    own = row_ref[0]

    @pl.when(pl.program_id(0) == 0)
    def _():
        nw_ref[...] = jnp.zeros_like(nw_ref)
        hs_ref[...] = jnp.zeros_like(hs_ref)

    h_out[...] = sweep_body(c_own, c_par, wb_ref, wbt_ref, ws_ref[...], h_ref[...], own, 1 - own, nw_ref, hs_ref)


def params():
    return pltpu.CompilerParams(vmem_limit_bytes=VMEM, dimension_semantics=("arbitrary",))


def cost(docs, columns, topics, dots):
    return pl.CostEstimate(flops=int(2 * docs * columns * topics * dots), bytes_accessed=2 * docs * columns, transcendentals=0)


def whole(shape):
    return pl.BlockSpec(shape, lambda j, row: (0,) * len(shape))


def solution(mesh):
    rows, cols = mesh.shape["row"], mesh.shape["col"]

    def body(counts, w_own, h_blk):
        docs, width = counts.shape
        topics = w_own.shape[1]
        mine = width // rows
        blocks = mine // BV
        row = lax.axis_index("row")
        row_arr = row.astype(jnp.int32).reshape(1)
        swap = [(0, 1), (1, 0)]
        sds = jax.ShapeDtypeStruct
        lanes = (topics, 128)

        recv = []
        for j in range(blocks):
            piece = lax.dynamic_slice(counts, (0, (1 - row) * mine + j * BV), (docs, BV))
            recv.append(lax.ppermute(piece, "row", swap))

        w_all = lax.all_gather(w_own, "row")
        h_mine = lax.dynamic_slice(h_blk, (0, row * mine), (topics, mine))

        def forms(w):
            wb = w.astype(BF16)
            return wb, jnp.swapaxes(wb, 1, 2), jnp.sum(w, axis=(0, 1))[:, None]

        wb0, wbt0, ws0 = forms(w_all)
        wb_own = w_own.astype(BF16)

        def place(j, row):
            return jnp.where(j < blocks, row[0] * blocks + j, (1 - row[0]) * blocks + j - blocks)

        nw, nh1, hs0 = pl.pallas_call(
            first_kernel,
            grid_spec=pltpu.PrefetchScalarGridSpec(
                num_scalar_prefetch=1, grid=(rows * blocks,),
                in_specs=[
                    pl.BlockSpec((docs, BV), lambda j, row: (0, place(j, row))),
                    whole((docs, topics)), whole((topics, docs)),
                    pl.BlockSpec((topics, BV), lambda j, row: (0, place(j, row))),
                ],
                out_specs=[
                    whole((docs, topics)),
                    pl.BlockSpec((topics, BV), lambda j, row: (0, jnp.minimum(j, blocks - 1))),
                    whole(lanes),
                ]),
            out_shape=[sds((docs, topics), F32), sds((topics, mine), F32), sds(lanes, F32)],
            compiler_params=params(), cost_estimate=cost(docs, width, topics, 2.5), name="first",
        )(row_arr, counts, wb_own, wb_own.T, h_blk)

        def total(nw, hs):
            both = jnp.concatenate([nw.reshape(rows * docs, topics), jnp.tile(jnp.sum(hs, axis=1)[None, :], (8, 1))], axis=0)
            both = lax.psum(both, ("row", "col"))
            return both[:rows * docs].reshape(rows, docs, topics), both[rows * docs]

        nw_all = jnp.where(lax.broadcasted_iota(jnp.int32, (rows, 1, 1), 0) == row, nw[None], 0.0)
        nw_all, hs = total(nw_all, jnp.where(row == 0, hs0, 0.0))
        w = w_all * nw_all / hs[None, None, :]
        wb1, wbt1, ws1 = forms(w)

        nw = jnp.zeros((rows, docs, topics), F32)
        hs1 = jnp.zeros(lanes, F32)
        hs2 = jnp.zeros(lanes, F32)
        h_parts = []
        for j in range(blocks):
            h_new, nw, hs1, hs2 = pl.pallas_call(
                chunk_kernel,
                grid_spec=pltpu.PrefetchScalarGridSpec(
                    num_scalar_prefetch=1, grid=(1,),
                    in_specs=[
                        pl.BlockSpec((docs, BV), lambda i, row, j=j: (0, row[0] * blocks + j)),
                        whole((docs, BV)),
                        whole((rows, docs, topics)), whole((rows, topics, docs)), whole((topics, 1)),
                        whole((rows, docs, topics)), whole((rows, topics, docs)), whole((topics, 1)),
                        pl.BlockSpec((topics, BV), lambda i, row, j=j: (0, j)),
                        pl.BlockSpec((topics, BV), lambda i, row, j=j: (0, j)),
                        whole((rows, docs, topics)), whole(lanes), whole(lanes),
                    ],
                    out_specs=[whole((topics, BV)), whole((rows, docs, topics)), whole(lanes), whole(lanes)]),
                out_shape=[sds((topics, BV), F32), sds((rows, docs, topics), F32), sds(lanes, F32), sds(lanes, F32)],
                compiler_params=params(), cost_estimate=cost(docs, BV, topics, 8), name=f"chunk{j}",
            )(row_arr, counts, recv[j], wb0, wbt0, ws0, wb1, wbt1, ws1, h_mine, nh1, nw, hs1, hs2)
            h_parts.append(h_new)

        c_par = jnp.concatenate(recv, axis=1)
        h = jnp.concatenate(h_parts, axis=1)
        nw, hs = total(nw, hs1)
        w = w * nw / hs[None, None, :]
        hs_next = hs2

        def sweep(w, h, start, count):
            wb, wbt, ws = forms(w)
            return pl.pallas_call(
                sweep_kernel,
                grid_spec=pltpu.PrefetchScalarGridSpec(
                    num_scalar_prefetch=1, grid=(count,),
                    in_specs=[
                        pl.BlockSpec((docs, BV), lambda j, row: (0, row[0] * blocks + start + j)),
                        pl.BlockSpec((docs, BV), lambda j, row: (0, start + j)),
                        whole((rows, docs, topics)), whole((rows, topics, docs)), whole((topics, 1)),
                        pl.BlockSpec((topics, BV), lambda j, row: (0, start + j)),
                    ],
                    out_specs=[pl.BlockSpec((topics, BV), lambda j, row: (0, j)), whole((rows, docs, topics)), whole(lanes)]),
                out_shape=[sds((topics, count * BV), F32), sds((rows, docs, topics), F32), sds(lanes, F32)],
                compiler_params=params(), cost_estimate=cost(docs, count * BV, topics, 6), name="sweep",
            )(row_arr, counts, c_par, wb, wbt, ws, h)

        for sweep_idx in range(2, SWEEPS - 1):
            h, nw, hs_new = sweep(w, h, 0, blocks)
            nw, hs = total(nw, hs_next)
            w = w * nw / hs[None, None, :]
            hs_next = hs_new

        step = 2
        nw_sum = jnp.zeros((rows, docs, topics), F32)
        h_out = jnp.zeros((topics, width), F32)
        for start in range(0, blocks, step):
            h_piece, nw, _ = sweep(w, h, start, step)
            nw_sum = nw_sum + nw
            other = lax.ppermute(h_piece, "row", swap)
            h_out = lax.dynamic_update_slice(h_out, h_piece, (0, row * mine + start * BV))
            h_out = lax.dynamic_update_slice(h_out, other, (0, (1 - row) * mine + start * BV))
        nw, hs = total(nw_sum, hs_next)
        w = w * nw / hs[None, None, :]
        w_out = lax.dynamic_slice(w, (row, 0, 0), (1, docs, topics))[0]
        return w_out, h_out

    return jax.shard_map(
        body,
        mesh=mesh,
        in_specs=(P(("part", "row"), "col"), P(("part", "row"), None), P("part", "col")),
        out_specs=(P(("part", "row"), None), P("part", "col")),
        check_vma=False,
    )
```

time: 2850 us -> 1100 us (0.39)
  waiting for transfers between devices: 2180 us -> 614 us
  matrix products: 447 us -> 0 us
  Pallas kernels: 0 us -> 276 us
  local copies, waits for them, and re-layouts: 34.9 us -> 135 us
  other arithmetic: 122 us -> 44.7 us
  blocking collectives: 48.9 us -> 0 us
    psum x12 -> x6, waiting for transfers between devices: 2180 us -> 308 us  [total(): both = lax.psum(both, ('row', 'col'))]
    dot_general x18 -> x0, matrix products: 447 us -> none  [the longest x6 187 us: local_sweeps(): z_local = jnp.dot(w_bf, h_bf, preferred_element_type=jnp.float32)]
    ppermute x0 -> x12, waiting for transfers between devices: none -> 306 us  [the longest x8 203 us: body(): recv.append(lax.ppermute(piece, 'row', swap))]
    pallas_call x0 -> x16, Pallas kernels: none -> 276 us  [the longest x7 151 us: sweep(): pl.pallas_call(sweep_kernel, grid_spec=pltpu.PrefetchScalarGridSpec(num_s...]
    reduce_sum x12 -> x11, other arithmetic: 102 us -> 12.9 us  [the longest x5 10.5 us: forms(): return (wb, jnp.swapaxes(wb, 1, 2), jnp.sum(w, axis=(0, 1))[:, None])]
    psum x7 -> x0, blocking collectives: 48.9 us -> none  [the longest x4 30.1 us: local_sweeps(): w_colsum = lax.psum(w_colsum, 'row')]
  transfers between devices with their start and end apart: 12 -> 19, of which waited for: 12 -> 16; matrix products, arithmetic and copies ran while one was open for 8% -> 9% of each run, Pallas kernels for 0% -> 7%
where the time goes in v1:
time: 1100 us
  waiting for transfers between devices  614 us (56%)
  Pallas kernels  276 us (25%)
  local copies, waits for them, and re-layouts  135 us (12%)
  other arithmetic  44.7 us (4%)
  between operations  16.1 us (1%)
  starting transfers between devices  12.1 us (1%)
    psum x6, waiting for transfers between devices, total(): both = lax.psum(both, ('row', 'col'))  308 us
    ppermute x8, waiting for transfers between devices, body(): recv.append(lax.ppermute(piece, 'row', swap))  203 us
    pallas_call x7, Pallas kernels, sweep(): pl.pallas_call(sweep_kernel, grid_spec=pltpu.PrefetchScalarGridSpec(num_s...  151 us
    ppermute x4, waiting for transfers between devices, body(): other = lax.ppermute(h_piece, 'row', swap)  103 us
    pallas_call x8, Pallas kernels, body(): pl.pallas_call(chunk_kernel, grid_spec=pltpu.PrefetchScalarGridSpec(num_s...  90.4 us
    unnamed x78, local copies, waits for them, and re-layouts  36.9 us
    pallas_call x1, Pallas kernels, body(): pl.pallas_call(first_kernel, grid_spec=pltpu.PrefetchScalarGridSpec(num_s...  34.2 us
  transfers between devices with their start and end apart: 19, of which 16 were waited for; matrix products, arithmetic and copies ran while one was open for 9% of the time, Pallas kernels for 7%

profile of v1, /device:TPU:0, one launch (start us, length us, event | category | flops | bytes accessed | tf_op | source)
XLA Modules:
  0.0 1098.4 jit_solution(13481826952723692214)
XLA Ops:
  10.6 34.2 %first.1 = (f32[1024,256]{1,0:T(8,128)}, f32[256,8192]{1,0:T(8,128)}, f32[256,128]{1,0:T(8,128)}) custom-call(s32[1]{0:T(128)} %bitcast.row_ref, bf16[1024,16384]{1,0:T(8,128)(2,1)} %c_own.29, bf16[1024,256]{1,0:T(8,128)(2,1)} %copy.31.wb_ref, bf16[256,1024]{1,0:T(8,128)(2,1)} %bitcast.73, f32[256,16384]{1,0:T(8,128)} %h_ref.1), custom_call_target="tpu_custom_call" | custom-call | flops 21474836480 | bytes 33554432 | tf_op jit(solution)/shard_map/first/pallas_call | solution.py:139
  49.6 12.3 %constant_dynamic-slice_fusion.9 = (bf16[1024,1024]{1,0:T(8,128)(2,1)}, bf16[1024,1024]{1,0:T(8,128)(2,1)}, bf16[1024,1024]{1,0:T(8,128)(2,1)}, bf16[1024,1024]{...) fusion(bf16[1024,16384]{1,0:T(8,128)(2,1)} %c_own.29, ...), kind=kLoop, calls=%fused_computation.50 | loop fusion | bytes 33554464 | tf_op jit(solution)/shard_map/dynamic_slice | solution.py:123
  68.4 7.6 constant_dynamic-slice_fusion.8.h_ref
  76.0 82.4 %all-reduce.7.cloned.1.call-done = f32[2056,256]{1,0:T(8,128)} async-done(((f32[2056,256]{1,0:T(8,128)}), f32[2056,256]{1,0:T(8,128)}) %all-reduce.7.cloned.1.call-update) | async-done | bytes 2105360 | tf_op jit(solution)/shard_map/psum | solution.py:159
  159.1 4.6 slice_multiply_fusion
  163.7 3.3 copy.32
  174.8 17.1 %collective-permute-done.6.c_par = bf16[1024,1024]{1,0:T(8,128)(2,1)} collective-permute-done((bf16[1024,1024]{1,0:T(8,128)(2,1)}, bf16[1024,1024]{1,0:T(8,128)(2,1)}, u32[]{:S(2)}, u32[]{:S(2)}) %collective-permute-start.6) | collective-permute-done | bytes 2097184 | tf_op jit(solution)/shard_map/ppermute | solution.py:124
  194.7 11.2 %chunk0.1 = (f32[256,1024]{1,0:T(8,128)}, f32[2,1024,256]{2,1,0:T(8,128)}, f32[256,128]{1,0:T(8,128)}, f32[256,128]{1,0:T(8,128)}) custom-call(s32[1]{0:T(128)} %bitcast.row_ref, bf16[1024,16384]{1,0:T(8,128)(2,1)} %c_own.29, bf16[1024,1024]{1,0:T(8,128)(2,1)} %copy-done.8, bf16[2,1024,256]{2,1,0:T(8,128)(2,1)} %bitcast.40, bf16[2,256,1024]{2,1,0:T(8,128)(2,1)} %bitcast.56, ...), custom_call_target="tpu_custom_call" | custom-call | flops 4294967296 | bytes 2097152 | tf_op jit(solution)/shard_map/chunk0/pallas_call | solution.py:172
  205.9 31.0 %collective-permute-done.5.c_par = bf16[1024,1024]{1,0:T(8,128)(2,1)} collective-permute-done((bf16[1024,1024]{1,0:T(8,128)(2,1)}, bf16[1024,1024]{1,0:T(8,128)(2,1)}, u32[]{:S(2)}, u32[]{:S(2)}) %collective-permute-start.5) | collective-permute-done | bytes 2097184 | tf_op jit(solution)/shard_map/ppermute | solution.py:124
  237.5 11.2 %chunk1.1 = (f32[256,1024]{1,0:T(8,128)}, f32[2,1024,256]{2,1,0:T(8,128)}, f32[256,128]{1,0:T(8,128)}, f32[256,128]{1,0:T(8,128)}) custom-call(s32[1]{0:T(128)} %bitcast.row_ref, bf16[1024,16384]{1,0:T(8,128)(2,1)} %c_own.29, bf16[1024,1024]{1,0:T(8,128)(2,1)} %collective-permute-done.6.c_par, bf16[2,1024,256]{2,1,0:T(8,128)(2,1)} %bitcast.41, ...), custom_call_target="tpu_custom_call" | custom-call | flops 4294967296 | bytes 2097152 | tf_op jit(solution)/shard_map/chunk1/pallas_call | solution.py:172
  248.7 11.4 %chunk2.1 = (f32[256,1024]{1,0:T(8,128)}, f32[2,1024,256]{2,1,0:T(8,128)}, f32[256,128]{1,0:T(8,128)}, f32[256,128]{1,0:T(8,128)}) custom-call(s32[1]{0:T(128)} %bitcast.row_ref, bf16[1024,16384]{1,0:T(8,128)(2,1)} %c_own.29, bf16[1024,1024]{1,0:T(8,128)(2,1)} %collective-permute-done.5.c_par, bf16[2,1024,256]{2,1,0:T(8,128)(2,1)} %bitcast.42, ...), custom_call_target="tpu_custom_call" | custom-call | flops 4294967296 | bytes 2097152 | tf_op jit(solution)/shard_map/chunk2/pallas_call | solution.py:172
  260.2 21.7 %collective-permute-done.4.c_par = bf16[1024,1024]{1,0:T(8,128)(2,1)} collective-permute-done((bf16[1024,1024]{1,0:T(8,128)(2,1)}, bf16[1024,1024]{1,0:T(8,128)(2,1)}, u32[]{:S(2)}, u32[]{:S(2)}) %collective-permute-start.4) | collective-permute-done | bytes 2097184 | tf_op jit(solution)/shard_map/ppermute | solution.py:124
  281.9 11.2 %chunk3.1 = (f32[256,1024]{1,0:T(8,128)}, f32[2,1024,256]{2,1,0:T(8,128)}, f32[256,128]{1,0:T(8,128)}, f32[256,128]{1,0:T(8,128)}) custom-call(s32[1]{0:T(128)} %bitcast.row_ref, bf16[1024,16384]{1,0:T(8,128)(2,1)} %c_own.29, bf16[1024,1024]{1,0:T(8,128)(2,1)} %collective-permute-done.4.c_par, bf16[2,1024,256]{2,1,0:T(8,128)(2,1)} %bitcast.43, ...), custom_call_target="tpu_custom_call" | custom-call | flops 4294967296 | bytes 2097152 | tf_op jit(solution)/shard_map/chunk3/pallas_call | solution.py:172
  293.1 33.7 %collective-permute-done.3.c_par = bf16[1024,1024]{1,0:T(8,128)(2,1)} collective-permute-done((bf16[1024,1024]{1,0:T(8,128)(2,1)}, bf16[1024,1024]{1,0:T(8,128)(2,1)}, u32[]{:S(2)}, u32[]{:S(2)}) %collective-permute-start.3) | collective-permute-done | bytes 2097184 | tf_op jit(solution)/shard_map/ppermute | solution.py:124
  326.8 11.6 %chunk4.1 = (f32[256,1024]{1,0:T(8,128)}, f32[2,1024,256]{2,1,0:T(8,128)}, f32[256,128]{1,0:T(8,128)}, f32[256,128]{1,0:T(8,128)}) custom-call(s32[1]{0:T(128)} %bitcast.row_ref, bf16[1024,16384]{1,0:T(8,128)(2,1)} %c_own.29, bf16[1024,1024]{1,0:T(8,128)(2,1)} %collective-permute-done.3.c_par, bf16[2,1024,256]{2,1,0:T(8,128)(2,1)} %bitcast.44, ...), custom_call_target="tpu_custom_call" | custom-call | flops 4294967296 | bytes 2097152 | tf_op jit(solution)/shard_map/chunk4/pallas_call | solution.py:172
  338.3 33.4 %collective-permute-done.2.c_par = bf16[1024,1024]{1,0:T(8,128)(2,1)} collective-permute-done((bf16[1024,1024]{1,0:T(8,128)(2,1)}, bf16[1024,1024]{1,0:T(8,128)(2,1)}, u32[]{:S(2)}, u32[]{:S(2)}) %collective-permute-start.2) | collective-permute-done | bytes 2097184 | tf_op jit(solution)/shard_map/ppermute | solution.py:124
  371.7 11.2 %chunk5.1 = (f32[256,1024]{1,0:T(8,128)}, f32[2,1024,256]{2,1,0:T(8,128)}, f32[256,128]{1,0:T(8,128)}, f32[256,128]{1,0:T(8,128)}) custom-call(s32[1]{0:T(128)} %bitcast.row_ref, bf16[1024,16384]{1,0:T(8,128)(2,1)} %c_own.29, bf16[1024,1024]{1,0:T(8,128)(2,1)} %collective-permute-done.2.c_par, bf16[2,1024,256]{2,1,0:T(8,128)(2,1)} %bitcast.45, ...), custom_call_target="tpu_custom_call" | custom-call | flops 4294967296 | bytes 2097152 | tf_op jit(solution)/shard_map/chunk5/pallas_call | solution.py:172
  382.9 33.8 %collective-permute-done.1.c_par = bf16[1024,1024]{1,0:T(8,128)(2,1)S(1)} collective-permute-done((bf16[1024,1024]{1,0:T(8,128)(2,1)}, bf16[1024,1024]{1,0:T(8,128)(2,1)S(1)}, u32[]{:S(2)}, u32[]{:S(2)}) %collective-permute-start.1) | collective-permute-done | bytes 2097184 | tf_op jit(solution)/shard_map/ppermute | solution.py:124
  418.1 11.2 %chunk6.1 = (f32[256,1024]{1,0:T(8,128)}, f32[2,1024,256]{2,1,0:T(8,128)}, f32[256,128]{1,0:T(8,128)}, f32[256,128]{1,0:T(8,128)}) custom-call(s32[1]{0:T(128)} %bitcast.row_ref, bf16[1024,16384]{1,0:T(8,128)(2,1)} %c_own.29, bf16[1024,1024]{1,0:T(8,128)(2,1)} %copy-done.10, bf16[2,1024,256]{2,1,0:T(8,128)(2,1)} %bitcast.46, bf16[2,256,1024]{2,1,0:T(8,128)(2,1)} %bitcast.62, ...), custom_call_target="tpu_custom_call" | custom-call | flops 4294967296 | bytes 2097152 | tf_op jit(solution)/shard_map/chunk6/pallas_call | solution.py:172
  429.3 32.2 %collective-permute-done.c_par = bf16[1024,1024]{1,0:T(8,128)(2,1)} collective-permute-done((bf16[1024,1024]{1,0:T(8,128)(2,1)}, bf16[1024,1024]{1,0:T(8,128)(2,1)}, u32[]{:S(2)}, u32[]{:S(2)}) %collective-permute-start) | collective-permute-done | bytes 2097184 | tf_op jit(solution)/shard_map/ppermute | solution.py:124
  461.4 11.4 %chunk7.1 = (f32[256,1024]{1,0:T(8,128)}, f32[2,1024,256]{2,1,0:T(8,128)}, f32[256,128]{1,0:T(8,128)}, f32[256,128]{1,0:T(8,128)}) custom-call(s32[1]{0:T(128)} %bitcast.row_ref, bf16[1024,16384]{1,0:T(8,128)(2,1)} %c_own.29, bf16[1024,1024]{1,0:T(8,128)(2,1)} %collective-permute-done.c_par, bf16[2,1024,256]{2,1,0:T(8,128)(2,1)} %bitcast.47, ...), custom_call_target="tpu_custom_call" | custom-call | flops 4294967296 | bytes 2097152 | tf_op jit(solution)/shard_map/chunk7/pallas_call | solution.py:172
  484.2 3.2 constant_dynamic-update-slice_fusion.6
  487.5 3.3 copy-done.24
  500.2 3.2 constant_dynamic-update-slice_fusion.2
  508.0 19.2 %all-reduce.9.cloned.1.call-done = f32[2056,256]{1,0:T(8,128)} async-done(((f32[2056,256]{1,0:T(8,128)}), f32[2056,256]{1,0:T(8,128)}) %all-reduce.9.cloned.1.call-update) | async-done | bytes 2105360 | tf_op jit(solution)/shard_map/psum | solution.py:159
  536.6 33.6 %sweep.7 = (f32[256,8192]{1,0:T(8,128)}, f32[2,1024,256]{2,1,0:T(8,128)}, f32[256,128]{1,0:T(8,128)}) custom-call(s32[1]{0:T(128)} %bitcast.row_ref, bf16[1024,16384]{1,0:T(8,128)(2,1)} %c_own.29, bf16[1024,8192]{1,0:T(8,128)(2,1)} %constant_dynamic-update-slice_fusion.c_par, bf16[2,1024,256]{2,1,0:T(8,128)(2,1)} %copy.59.wb_ref, ...), custom_call_target="tpu_custom_call" | custom-call | flops 25769803776 | bytes 16777216 | tf_op jit(solution)/shard_map/sweep/pallas_call | solution.py:199
  570.2 3.1 pad_maximum_fusion.2
  574.4 48.9 %all-reduce.11.cloned.1.call-done = f32[2056,256]{1,0:T(8,128)} async-done(((f32[2056,256]{1,0:T(8,128)}), f32[2056,256]{1,0:T(8,128)}) %all-reduce.11.cloned.1.call-update) | async-done | bytes 2105360 | tf_op jit(solution)/shard_map/psum | solution.py:159
  626.4 3.2 copy.61
  635.2 33.5 %sweep.8 = (f32[256,8192]{1,0:T(8,128)}, f32[2,1024,256]{2,1,0:T(8,128)}, f32[256,128]{1,0:T(8,128)}) custom-call(s32[1]{0:T(128)} %bitcast.row_ref, bf16[1024,16384]{1,0:T(8,128)(2,1)} %c_own.29, bf16[1024,8192]{1,0:T(8,128)(2,1)} %constant_dynamic-update-slice_fusion.c_par, bf16[2,1024,256]{2,1,0:T(8,128)(2,1)} %copy.62.wb_ref, ...), custom_call_target="tpu_custom_call" | custom-call | flops 25769803776 | bytes 16777216 | tf_op jit(solution)/shard_map/sweep/pallas_call | solution.py:199
  672.8 49.0 %all-reduce.13.cloned.1.call-done = f32[2056,256]{1,0:T(8,128)} async-done(((f32[2056,256]{1,0:T(8,128)}), f32[2056,256]{1,0:T(8,128)}) %all-reduce.13.cloned.1.call-update) | async-done | bytes 2105360 | tf_op jit(solution)/shard_map/psum | solution.py:159
  733.6 33.5 %sweep.9 = (f32[256,8192]{1,0:T(8,128)}, f32[2,1024,256]{2,1,0:T(8,128)}, f32[256,128]{1,0:T(8,128)}) custom-call(s32[1]{0:T(128)} %bitcast.row_ref, bf16[1024,16384]{1,0:T(8,128)(2,1)} %c_own.29, bf16[1024,8192]{1,0:T(8,128)(2,1)} %constant_dynamic-update-slice_fusion.c_par, bf16[2,1024,256]{2,1,0:T(8,128)(2,1)} %copy.65.wb_ref, ...), custom_call_target="tpu_custom_call" | custom-call | flops 25769803776 | bytes 16777216 | tf_op jit(solution)/shard_map/sweep/pallas_call | solution.py:199
  771.2 48.9 %all-reduce.15.cloned.1.call-done = f32[2056,256]{1,0:T(8,128)} async-done(((f32[2056,256]{1,0:T(8,128)}), f32[2056,256]{1,0:T(8,128)}) %all-reduce.15.cloned.1.call-update) | async-done | bytes 2105360 | tf_op jit(solution)/shard_map/psum | solution.py:159
  823.2 3.5 copy.67
  832.4 12.6 %sweep.13 = (f32[256,2048]{1,0:T(8,128)}, f32[2,1024,256]{2,1,0:T(8,128)}, f32[256,128]{1,0:T(8,128)}) custom-call(s32[1]{0:T(128)} %bitcast.row_ref, bf16[1024,16384]{1,0:T(8,128)(2,1)} %c_own.29, bf16[1024,8192]{1,0:T(8,128)(2,1)} %constant_dynamic-update-slice_fusion.c_par, bf16[2,1024,256]{2,1,0:T(8,128)(2,1)} %copy.68.wb_ref, ...), custom_call_target="tpu_custom_call" | custom-call | flops 6442450944 | bytes 4194304 | tf_op jit(solution)/shard_map/sweep/pallas_call | solution.py:199
  845.0 12.6 %sweep.12 = (f32[256,2048]{1,0:T(8,128)}, f32[2,1024,256]{2,1,0:T(8,128)}, f32[256,128]{1,0:T(8,128)}) custom-call(s32[1]{0:T(128)} %bitcast.row_ref, bf16[1024,16384]{1,0:T(8,128)(2,1)} %c_own.29, bf16[1024,8192]{1,0:T(8,128)(2,1)} %constant_dynamic-update-slice_fusion.c_par, bf16[2,1024,256]{2,1,0:T(8,128)(2,1)} %copy.68.wb_ref, ...), custom_call_target="tpu_custom_call" | custom-call | flops 6442450944 | bytes 4194304 | tf_op jit(solution)/shard_map/sweep/pallas_call | solution.py:199
  857.6 12.6 %sweep.11 = (f32[256,2048]{1,0:T(8,128)}, f32[2,1024,256]{2,1,0:T(8,128)}, f32[256,128]{1,0:T(8,128)}) custom-call(s32[1]{0:T(128)} %bitcast.row_ref, bf16[1024,16384]{1,0:T(8,128)(2,1)} %c_own.29, bf16[1024,8192]{1,0:T(8,128)(2,1)} %constant_dynamic-update-slice_fusion.c_par, bf16[2,1024,256]{2,1,0:T(8,128)(2,1)} %copy.68.wb_ref, ...), custom_call_target="tpu_custom_call" | custom-call | flops 6442450944 | bytes 4194304 | tf_op jit(solution)/shard_map/sweep/pallas_call | solution.py:199
  870.2 12.8 %sweep.10 = (f32[256,2048]{1,0:T(8,128)}, f32[2,1024,256]{2,1,0:T(8,128)}, f32[256,128]{1,0:T(8,128)}) custom-call(s32[1]{0:T(128)} %bitcast.row_ref, bf16[1024,16384]{1,0:T(8,128)(2,1)} %c_own.29, bf16[1024,8192]{1,0:T(8,128)(2,1)} %constant_dynamic-update-slice_fusion.c_par, bf16[2,1024,256]{2,1,0:T(8,128)(2,1)} %copy.68.wb_ref, ...), custom_call_target="tpu_custom_call" | custom-call | flops 6442450944 | bytes 4194304 | tf_op jit(solution)/shard_map/sweep/pallas_call | solution.py:199
  885.1 3.4 add_add_fusion
  892.1 8.1 broadcast_in_dim.72
  901.7 59.5 %all-reduce.17.cloned.1.call-done = f32[2056,256]{1,0:T(8,128)} async-done(((f32[2056,256]{1,0:T(8,128)}), f32[2056,256]{1,0:T(8,128)}) %all-reduce.17.cloned.1.call-update) | async-done | bytes 2105360 | tf_op jit(solution)/shard_map/psum | solution.py:159
  967.4 32.1 %collective-permute-done.8 = f32[256,2048]{1,0:T(8,128)} collective-permute-done((f32[256,2048]{1,0:T(8,128)}, f32[256,2048]{1,0:T(8,128)}, u32[]{:S(2)}, u32[]{:S(2)}) %collective-permute-start.8) | collective-permute-done | bytes 2097184 | tf_op jit(solution)/shard_map/ppermute | solution.py:226
  999.5 3.1 constant_dynamic-update-slice_fusion.22
  1004.1 3.1 constant_dynamic-update-slice_fusion.20
  1010.4 34.1 %collective-permute-done.10 = f32[256,2048]{1,0:T(8,128)} collective-permute-done((f32[256,2048]{1,0:T(8,128)}, f32[256,2048]{1,0:T(8,128)}, u32[]{:S(2)}, u32[]{:S(2)}) %collective-permute-start.10) | collective-permute-done | bytes 2097184 | tf_op jit(solution)/shard_map/ppermute | solution.py:226
  1044.5 3.1 constant_dynamic-update-slice_fusion.18
  1050.7 36.9 %collective-permute-done.11 = f32[256,2048]{1,0:T(8,128)} collective-permute-done((f32[256,2048]{1,0:T(8,128)}, f32[256,2048]{1,0:T(8,128)}, u32[]{:S(2)}, u32[]{:S(2)}) %collective-permute-start.11) | collective-permute-done | bytes 2097184 | tf_op jit(solution)/shard_map/ppermute | solution.py:226
  1087.6 3.1 constant_dynamic-update-slice_fusion.16
  (182 shorter events, 121.4 us)
Async XLA Ops:
  8.0 150.5 %all-reduce.7.cloned.1.call-start = ((), (), s32[]{:S(2)}) async-start(), calls=%async_computation | async-start | bytes 4210688 | tf_op jit(solution)/shard_map/psum | solution.py:159
  48.9 110.2 %all-gather.3.cloned.1.call-start = ((), (), s32[]{:S(2)}) async-start(), calls=%async_computation.6 | async-start | bytes 3145728 | tf_op jit(solution)/shard_map/all_gather | solution.py:126
  49.5 477.6 %all-reduce.9.cloned.1.call-start = ((), (), s32[]{:S(2)}) async-start(), calls=%async_computation.1 | async-start | bytes 4210688 | tf_op jit(solution)/shard_map/psum | solution.py:159
  61.9 105.1 %collective-permute-start.7 = (bf16[1024,1024]{1,0:T(8,128)(2,1)}, bf16[1024,1024]{1,0:T(8,128)(2,1)S(1)}, u32[]{:S(2)}, u32[]{:S(2)}) collective-permute-start(bf16[1024,1024]{1,0:T(8,128)(2,1)} %get-tuple-element.115), channel_id=1, source_target_pairs={{0,4},{4,0},{1,5},{5,1},{2,6},{6,2},{3,7},{7,3}} | collective-permute-start | bytes 6291464 | tf_op jit(solution)/shard_map/ppermute | solution.py:124
  64.4 127.6 %collective-permute-start.6 = (bf16[1024,1024]{1,0:T(8,128)(2,1)}, bf16[1024,1024]{1,0:T(8,128)(2,1)}, u32[]{:S(2)}, u32[]{:S(2)}) collective-permute-start(bf16[1024,1024]{1,0:T(8,128)(2,1)} %get-tuple-element.116), channel_id=1, source_target_pairs={{0,4},{4,0},{1,5},{5,1},{2,6},{6,2},{3,7},{7,3}} | collective-permute-start | bytes 6291464 | tf_op jit(solution)/shard_map/ppermute | solution.py:124
  64.4 172.5 %collective-permute-start.5 = (bf16[1024,1024]{1,0:T(8,128)(2,1)}, bf16[1024,1024]{1,0:T(8,128)(2,1)}, u32[]{:S(2)}, u32[]{:S(2)}) collective-permute-start(bf16[1024,1024]{1,0:T(8,128)(2,1)} %get-tuple-element.117), channel_id=1, source_target_pairs={{0,4},{4,0},{1,5},{5,1},{2,6},{6,2},{3,7},{7,3}} | collective-permute-start | bytes 6291464 | tf_op jit(solution)/shard_map/ppermute | solution.py:124
  66.4 215.5 %collective-permute-start.4 = (bf16[1024,1024]{1,0:T(8,128)(2,1)}, bf16[1024,1024]{1,0:T(8,128)(2,1)}, u32[]{:S(2)}, u32[]{:S(2)}) collective-permute-start(bf16[1024,1024]{1,0:T(8,128)(2,1)} %get-tuple-element.118), channel_id=1, source_target_pairs={{0,4},{4,0},{1,5},{5,1},{2,6},{6,2},{3,7},{7,3}} | collective-permute-start | bytes 6291464 | tf_op jit(solution)/shard_map/ppermute | solution.py:124
  66.4 260.4 %collective-permute-start.3 = (bf16[1024,1024]{1,0:T(8,128)(2,1)}, bf16[1024,1024]{1,0:T(8,128)(2,1)}, u32[]{:S(2)}, u32[]{:S(2)}) collective-permute-start(bf16[1024,1024]{1,0:T(8,128)(2,1)} %get-tuple-element.119), channel_id=1, source_target_pairs={{0,4},{4,0},{1,5},{5,1},{2,6},{6,2},{3,7},{7,3}} | collective-permute-start | bytes 6291464 | tf_op jit(solution)/shard_map/ppermute | solution.py:124
  159.1 9.2 copy-start.29
  163.7 7.5 copy-start
  167.0 1.3 copy-start.8
  167.0 204.7 %collective-permute-start.2 = (bf16[1024,1024]{1,0:T(8,128)(2,1)}, bf16[1024,1024]{1,0:T(8,128)(2,1)}, u32[]{:S(2)}, u32[]{:S(2)}) collective-permute-start(bf16[1024,1024]{1,0:T(8,128)(2,1)} %get-tuple-element.120), channel_id=1, source_target_pairs={{0,4},{4,0},{1,5},{5,1},{2,6},{6,2},{3,7},{7,3}} | collective-permute-start | bytes 6291464 | tf_op jit(solution)/shard_map/ppermute | solution.py:124
  170.3 4.6 copy-start.1
  192.0 224.7 %collective-permute-start.1 = (bf16[1024,1024]{1,0:T(8,128)(2,1)}, bf16[1024,1024]{1,0:T(8,128)(2,1)S(1)}, u32[]{:S(2)}, u32[]{:S(2)}) collective-permute-start(bf16[1024,1024]{1,0:T(8,128)(2,1)} %get-tuple-element.121), channel_id=1, source_target_pairs={{0,4},{4,0},{1,5},{5,1},{2,6},{6,2},{3,7},{7,3}} | collective-permute-start | bytes 6291464 | tf_op jit(solution)/shard_map/ppermute | solution.py:124
  236.9 224.5 %collective-permute-start = (bf16[1024,1024]{1,0:T(8,128)(2,1)}, bf16[1024,1024]{1,0:T(8,128)(2,1)}, u32[]{:S(2)}, u32[]{:S(2)}) collective-permute-start(bf16[1024,1024]{1,0:T(8,128)(2,1)} %get-tuple-element.114), channel_id=1, source_target_pairs={{0,4},{4,0},{1,5},{5,1},{2,6},{6,2},{3,7},{7,3}} | collective-permute-start | bytes 6291464 | tf_op jit(solution)/shard_map/ppermute | solution.py:124
  416.7 1.4 copy-start.10
  476.9 1.5 copy-start.17
  476.9 146.4 %all-reduce.11.cloned.1.call-start = ((), (), s32[]{:S(2)}) async-start(), calls=%async_computation.2 | async-start | bytes 4210688 | tf_op jit(solution)/shard_map/psum | solution.py:159
  478.1 1.3 copy-start.18
  481.0 1.7 copy-start.9
  484.2 3.2 copy-start.23
  487.4 3.5 copy-start.25
  487.5 3.3 copy-start.24
  500.2 3.2 copy-start.11
  527.2 1.6 slice-start
  528.7 1.8 slice-start.1
  528.7 1.8 copy-start.30
  573.4 148.3 %all-reduce.13.cloned.1.call-start = ((), (), s32[]{:S(2)}) async-start(), calls=%async_computation.3 | async-start | bytes 4210688 | tf_op jit(solution)/shard_map/psum | solution.py:159
  626.4 3.2 slice-start.4
  631.5 1.6 copy-start.2
  671.8 148.4 %all-reduce.15.cloned.1.call-start = ((), (), s32[]{:S(2)}) async-start(), calls=%async_computation.4 | async-start | bytes 4210688 | tf_op jit(solution)/shard_map/psum | solution.py:159
  724.8 3.1 copy-start.3
  724.8 3.1 slice-start.5
  729.9 1.6 copy-start.4
  770.2 190.9 %all-reduce.17.cloned.1.call-start = ((), (), s32[]{:S(2)}) async-start(), calls=%async_computation.5 | async-start | bytes 4210688 | tf_op jit(solution)/shard_map/psum | solution.py:159
  823.1 3.5 copy-start.5
  823.2 3.5 slice-start.6
  828.6 1.7 copy-start.6
  870.2 14.9 %copy-start.12 = (f32[2,1024,256]{2,1,0:T(8,128)S(1)}, f32[2,1024,256]{2,1,0:T(8,128)}, u32[]{:S(2)}) copy-start(f32[2,1024,256]{2,1,0:T(8,128)} %get-tuple-element.100) | copy-start | bytes 6291460
  883.0 121.1 %collective-permute-start.9 = (f32[256,2048]{1,0:T(8,128)}, f32[256,2048]{1,0:T(8,128)}, u32[]{:S(2)}, u32[]{:S(2)}) collective-permute-start(f32[256,2048]{1,0:T(8,128)} %get-tuple-element.103), channel_id=1, source_target_pairs={{0,4},{4,0},{1,5},{5,1},{2,6},{6,2},{3,7},{7,3}} | collective-permute-start | bytes 6291464 | tf_op jit(solution)/shard_map/ppermute | solution.py:226
  883.8 115.7 %collective-permute-start.8 = (f32[256,2048]{1,0:T(8,128)}, f32[256,2048]{1,0:T(8,128)}, u32[]{:S(2)}, u32[]{:S(2)}) collective-permute-start(f32[256,2048]{1,0:T(8,128)} %get-tuple-element.102), channel_id=1, source_target_pairs={{0,4},{4,0},{1,5},{5,1},{2,6},{6,2},{3,7},{7,3}} | collective-permute-start | bytes 6291464 | tf_op jit(solution)/shard_map/ppermute | solution.py:226
  890.0 154.4 %collective-permute-start.10 = (f32[256,2048]{1,0:T(8,128)}, f32[256,2048]{1,0:T(8,128)}, u32[]{:S(2)}, u32[]{:S(2)}) collective-permute-start(f32[256,2048]{1,0:T(8,128)} %get-tuple-element.104), channel_id=1, source_target_pairs={{0,4},{4,0},{1,5},{5,1},{2,6},{6,2},{3,7},{7,3}} | collective-permute-start | bytes 6291464 | tf_op jit(solution)/shard_map/ppermute | solution.py:226
  890.8 9.4 copy-start.15
  890.8 196.8 %collective-permute-start.11 = (f32[256,2048]{1,0:T(8,128)}, f32[256,2048]{1,0:T(8,128)}, u32[]{:S(2)}, u32[]{:S(2)}) collective-permute-start(f32[256,2048]{1,0:T(8,128)} %get-tuple-element.105), channel_id=1, source_target_pairs={{0,4},{4,0},{1,5},{5,1},{2,6},{6,2},{3,7},{7,3}} | collective-permute-start | bytes 6291464 | tf_op jit(solution)/shard_map/ppermute | solution.py:226
  961.1 1.6 slice-start.2
  962.7 2.0 copy-start.7
  962.7 2.0 slice-start.3
  967.4 35.2 %copy-start.14 = (f32[256,2048]{1,0:T(8,128)S(1)}, f32[256,2048]{1,0:T(8,128)}, u32[]{:S(2)}) copy-start(f32[256,2048]{1,0:T(8,128)} %get-tuple-element.103) | copy-start | bytes 6291460
  (9 other events, 10.1 us)
Sparse Core Ops, SparseCore 0:
  49.1 109.3 all-reduce.6
  477.0 50.0 all-reduce.8
  573.5 49.7 all-reduce.10
  671.9 49.7 all-reduce.12
  770.3 49.7 all-reduce.14
  890.2 70.9 all-reduce.16
Sparse Core Ops, SparseCore 1:
  50.9 53.3 all-gather.2

commit v2 on v0

v2 whole, which is shorter than its diff:
```python
import functools

import jax
import jax.numpy as jnp
from jax import lax
from jax.experimental import pallas as pl
from jax.experimental.pallas import tpu as pltpu
from jax.sharding import PartitionSpec as P

SWEEPS = 6
F32 = jnp.float32
BF16 = jnp.bfloat16
BV = 1024
VMEM = 60 * 1024 * 1024


def dot(a, b):
    return jnp.dot(a, b, preferred_element_type=F32)


def dot_t(a, b):
    return lax.dot_general(a, b, (((1,), (1,)), ((), ())), preferred_element_type=F32)


def ratio(c, z):
    return (c.astype(F32) / z).astype(BF16)


def lane_sum(h):
    out = h[:, :128]
    for g in range(1, h.shape[1] // 128):
        out = out + h[:, g * 128:(g + 1) * 128]
    return out


def sweep_body(c_own, c_par, wb_ref, wbt_ref, ws, h, own, par, nw_ref, hs_ref):
    hb = h.astype(BF16)
    q_own = ratio(c_own[...], dot(wb_ref[own], hb))
    nw_ref[own] += dot_t(q_own, hb)
    nh = dot(wbt_ref[own], q_own)
    q_par = ratio(c_par[...], dot(wb_ref[par], hb))
    nw_ref[par] += dot_t(q_par, hb)
    nh = nh + dot(wbt_ref[par], q_par)
    new = h * nh / ws
    hs_ref[...] += lane_sum(new)
    return new


def sweep_kernel(row_ref, c_own, c_par, wb_ref, wbt_ref, ws_ref, h_ref, h_out, nw_ref, hs_ref):
    own = row_ref[0]

    @pl.when(pl.program_id(0) == 0)
    def _():
        nw_ref[...] = jnp.zeros_like(nw_ref)
        hs_ref[...] = jnp.zeros_like(hs_ref)

    h_out[...] = sweep_body(c_own, c_par, wb_ref, wbt_ref, ws_ref[...], h_ref[...], own, 1 - own, nw_ref, hs_ref)

DEVICES = 8
EXTRA = 8
CHUNK = 512
AHEAD = 6
UPDATE_AT = 3


def main_kernel(sweeps, grid_cols, counts, w_in, h_in,
                c_par, h_ref, wb_ref, ws_ref, hs_acc, wsl_ref,
                cbuf, hbuf, nh_ref, wbt_ref, wb0, wbt0, ws0_buf, ws0_ref, hs_first, acc, nw_recv, ws_buf, ws_half, hs_row,
                csem, psem, hsem, hhsem, c_send, c_got, w0_send, w0_got,
                nw_send, nw_got, wb_send, wb_got, ws_send, ws_got):
    row, col = lax.axis_index("row"), lax.axis_index("col")
    me = row * grid_cols + col
    docs, full = counts.shape
    topics, width = h_ref.shape
    blocks = width // BV
    chunks = width // CHUNK
    part = docs // DEVICES
    partner = {"row": 1 - row, "col": col}
    mesh_id = pl.DeviceIdType.MESH

    def remote(src, dst, send, got, where):
        return pltpu.make_async_remote_copy(src, dst, send, got, device_id=where, device_id_type=mesh_id)

    def peer(p):
        other = lax.rem(me + p, DEVICES)
        return {"row": other // grid_cols, "col": lax.rem(other, grid_cols)}, other

    def nw_copy(p, half):
        where, other = peer(p)
        return remote(acc.at[half, other], nw_recv.at[half, p], nw_send.at[half, p], nw_got.at[half, p], where)

    def wb_copy(p, half):
        mine = wb_ref.at[half, pl.ds(pl.multiple_of(me * part, part), part)]
        return remote(mine, mine, wb_send.at[half, p], wb_got.at[half, p], peer(p)[0])

    def ws_copy(p, half):
        return remote(ws_buf.at[half, 0], ws_buf.at[half, p], ws_send.at[half, p], ws_got.at[half, p], peer(p)[0])

    def first_copy(q, cross):
        to_row_, to_col = (1 - row if cross else row), lax.rem(col + q, grid_cols)
        slot = int(cross)
        return remote(acc.at[row, to_row_ * grid_cols + to_col], nw_recv.at[row, q], nw_send.at[slot, q],
                      nw_got.at[row, q], {"row": to_row_, "col": to_col})

    def first_arrival(q, half):
        return remote(acc.at[0, 0], nw_recv.at[half, q], nw_send.at[0, q], nw_got.at[half, q], partner)

    def chunk_copy(j):
        theirs = pl.ds(pl.multiple_of((1 - row) * width + j * CHUNK, CHUNK), CHUNK)
        here = pl.ds(pl.multiple_of(j * CHUNK, CHUNK), CHUNK)
        return remote(counts.at[:, theirs], c_par.at[:, here], c_send.at[j], c_got.at[j], partner)

    def w0_copies():
        other = (1 - row) * grid_cols + col
        return [
            remote(wb0.at[0], wb0.at[1], w0_send.at[0], w0_got.at[0], partner),
            remote(ws0_buf.at[0], ws0_buf.at[1], w0_send.at[1], w0_got.at[1], partner),
            remote(w_in.at[pl.ds(pl.multiple_of(other * part, part), part)], wsl_ref.at[row], w0_send.at[2], w0_got.at[2],
                   partner),
        ]

    def local(src, dst, sem):
        return pltpu.make_async_copy(src, dst, sem)

    def c_start(half, j, slot):
        @pl.when(row == half)
        def _():
            local(counts.at[:, pl.ds(pl.multiple_of(row * width + j * BV, BV), BV)], cbuf.at[slot], csem.at[slot]).start()

        @pl.when(row != half)
        def _():
            local(c_par.at[:, pl.ds(pl.multiple_of(j * BV, BV), BV)], cbuf.at[slot], csem.at[slot]).start()

    def c_wait(slot):
        local(counts.at[:, pl.ds(0, BV)], cbuf.at[slot], csem.at[slot]).wait()

    def first_c(i, slot):
        block = lax.rem(row * blocks + i, 2 * blocks)
        return local(counts.at[:, pl.ds(pl.multiple_of(block * BV, BV), BV)], cbuf.at[slot], csem.at[slot])

    def first_h(j, slot):
        at = pl.ds(pl.multiple_of((1 - row) * width + j * BV, BV), BV)
        return local(h_in.at[:, at], hbuf.at[slot], hsem.at[slot])

    def own_chunk(j, slot):
        at = pl.ds(pl.multiple_of(row * width + j * CHUNK, CHUNK), CHUNK)
        return local(counts.at[:, at], cbuf.at[slot, :, pl.ds(0, CHUNK)], csem.at[slot])

    def par_chunk(j, slot):
        at = pl.ds(pl.multiple_of(j * CHUNK, CHUNK), CHUNK)
        return local(c_par.at[:, at], cbuf.at[slot, :, pl.ds(CHUNK, CHUNK)], psem)

    def acc_add(half, res):
        for b in range(DEVICES):
            acc[half, b, pl.ds(0, part)] += res[b * part:(b + 1) * part]

    def acc_sums(half):
        for b in range(DEVICES):
            acc[half, b, pl.ds(part, EXTRA)] = hs_row[...]

    def acc_zero(half):
        acc[half] = jnp.zeros(acc.shape[1:], F32)

    def send_nw(half):
        acc_sums(half)
        for p in range(1, DEVICES):
            nw_copy(p, half).start()

    def publish(half, total):
        new = wsl_ref[half] * total[:part] / total[part:part + 1]
        wsl_ref[half] = new
        wb_ref[half, pl.ds(pl.multiple_of(me * part, part), part)] = new.astype(BF16)
        ws_buf[half, 0] = jnp.broadcast_to(jnp.sum(new, axis=0, keepdims=True), (EXTRA, topics))
        for p in range(1, DEVICES):
            wb_copy(p, half).start()
            ws_copy(p, half).start()

    def sent_w(half):
        for p in range(1, DEVICES):
            wb_copy(p, half).wait_send()
            ws_copy(p, half).wait_send()

    def sent_nw(half):
        for p in range(1, DEVICES):
            nw_copy(p, half).wait_send()

    def owner_update(half):
        for p in range(1, DEVICES):
            nw_copy(p, half).wait_recv()
        total = acc[half, me]
        for p in range(1, DEVICES):
            total = total + nw_recv[half, p]
        sent_w(half)
        publish(half, total)

    def receive_w(half):
        for p in range(1, DEVICES):
            wb_copy(p, half).wait_recv()
            ws_copy(p, half).wait_recv()
        wbt_ref[half] = wb_ref[half].T
        total = ws_buf[half, 0]
        for p in range(1, DEVICES):
            total = total + ws_buf[half, p]
        return total

    def to_row(lanes):
        return jnp.broadcast_to(jnp.sum(lanes.T, axis=0, keepdims=True), (EXTRA, topics))

    def to_lanes(sums):
        return jnp.broadcast_to(sums[:1], (128, topics)).T

    barrier = pltpu.get_barrier_semaphore()
    for p in range(1, DEVICES):
        pl.semaphore_signal(barrier, inc=1, device_id=peer(p)[0], device_id_type=mesh_id)

    own_h = local(h_in.at[:, pl.ds(pl.multiple_of(row * width, width), width)], h_ref, hhsem)
    own_h.start()
    first_c(0, 0).start()
    wb0[0] = w_in[...].astype(BF16)
    ws0_buf[0] = jnp.broadcast_to(jnp.sum(w_in[...], axis=0, keepdims=True), (EXTRA, topics))
    wsl_ref[row] = w_in[pl.ds(pl.multiple_of(me * part, part), part)]
    pl.semaphore_wait(barrier, DEVICES - 1)
    for copy in w0_copies():
        copy.start()
    for j in range(AHEAD):
        chunk_copy(j).start()
    wbt0[0] = wb0[0].T
    acc_zero(0)
    acc_zero(1)
    hs_first[...] = jnp.zeros_like(hs_first)
    hs_acc[...] = jnp.zeros_like(hs_acc)
    own_h.wait()

    def first_own(j, carry):
        slot = lax.rem(j, 2)
        first_c(j, slot).wait()
        first_c(j + 1, 1 - slot).start()

        @pl.when(j == blocks - 1)
        def _():
            first_h(0, 0).start()

        at = pl.ds(pl.multiple_of(j * BV, BV), BV)
        h = h_ref[:, at]
        hb = h.astype(BF16)
        q = ratio(cbuf[slot], dot(wb0[0], hb))
        acc_add(row, dot_t(q, hb))
        nh_ref[:, at] = dot(wbt0[0], q)
        hs_first[...] += lane_sum(h)
        return carry

    lax.fori_loop(0, blocks, first_own, 0)

    def first_other(j, carry):
        slot = lax.rem(j, 2)
        first_c(blocks + j, slot).wait()
        first_h(j, slot).wait()

        @pl.when(j < blocks - 1)
        def _():
            first_c(blocks + j + 1, 1 - slot).start()
            first_h(j + 1, 1 - slot).start()

        h = hbuf[slot]
        hb = h.astype(BF16)
        q = ratio(cbuf[slot], dot(wb0[0], hb))
        acc_add(row, dot_t(q, hb))
        hs_first[...] += lane_sum(h)
        return carry

    lax.fori_loop(0, blocks, first_other, 0)

    hs_row[...] = to_row(hs_first[...])
    acc_sums(row)
    for q in range(grid_cols):
        first_copy(q, True).start()
        if q:
            first_copy(q, False).start()
    own_chunk(0, 0).start()
    for copy in w0_copies():
        copy.wait_recv()
    wbt0[1] = wb0[1].T
    ws0_ref[...] = to_lanes(ws0_buf[0] + ws0_buf[1])
    hs_first[...] = jnp.zeros_like(hs_first)
    total = acc[row, me]
    for q in range(1, grid_cols):
        first_arrival(q, row).wait_recv()
        total = total + nw_recv[row, q]
    publish(row, total)
    first_arrival(0, 1 - row).wait_recv()
    total = nw_recv[1 - row, 0]
    for q in range(1, grid_cols):
        first_arrival(q, 1 - row).wait_recv()
        total = total + nw_recv[1 - row, q]
    publish(1 - row, total)
    for q in range(grid_cols):
        first_copy(q, True).wait_send()
        if q:
            first_copy(q, False).wait_send()
    acc_zero(row)
    ws_ref[...] = to_lanes(receive_w(0) + receive_w(1))

    def chunk_step(j, carry):
        slot = lax.rem(j, 2)
        chunk_copy(j).wait_recv()
        par_chunk(j, slot).start()
        chunk_copy(j).wait_send()

        @pl.when(jnp.logical_and(j >= AHEAD - 2, j < chunks - 2))
        def _():
            chunk_copy(j + 2).start()

        own_chunk(j, slot).wait()

        @pl.when(j < chunks - 1)
        def _():
            own_chunk(j + 1, 1 - slot).start()

        at = pl.ds(pl.multiple_of(j * CHUNK, CHUNK), CHUNK)
        h = h_ref[:, at]
        par_chunk(j, slot).wait()
        other = cbuf[slot, :, pl.ds(CHUNK, CHUNK)]
        q = ratio(other, dot(wb0[1], h.astype(BF16)))
        h = h * (nh_ref[:, at] + dot(wbt0[1], q)) / ws0_ref[:, :1]
        hs_first[...] += lane_sum(h)
        hb = h.astype(BF16)
        q = ratio(cbuf[slot, :, pl.ds(0, CHUNK)], dot(wb_ref[row], hb))
        acc_add(row, dot_t(q, hb))
        nh = dot(wbt_ref[row], q)
        q = ratio(other, dot(wb_ref[1 - row], hb))
        acc_add(1 - row, dot_t(q, hb))
        nh = nh + dot(wbt_ref[1 - row], q)
        h = h * nh / ws_ref[:, :1]
        h_ref[:, at] = h
        hs_acc[...] += lane_sum(h)
        return carry

    lax.fori_loop(0, chunks, chunk_step, 0)
    for copy in w0_copies():
        copy.wait_send()
    hs_row[...] = to_row(hs_first[...])
    send_nw(0)
    send_nw(1)
    c_start(0, 0, 0)
    owner_update(0)

    def step(half, j, last):
        slot = lax.rem(j, 2)
        c_wait(slot)

        @pl.when(j < blocks - 1)
        def _():
            c_start(half, j + 1, 1 - slot)

        @pl.when(jnp.logical_and(j == blocks - 1, jnp.logical_not(last)))
        def _():
            c_start(1 - half, 0, 1 - slot)

        at = pl.ds(pl.multiple_of(j * BV, BV), BV)
        hb = h_ref[:, at].astype(BF16)
        q = ratio(cbuf[slot], dot(wb_ref[half], hb))
        acc_add(half, dot_t(q, hb))
        nh = dot(wbt_ref[half], q)
        if half == 0:
            nh_ref[:, at] = nh
        else:
            new = h_ref[:, at] * (nh_ref[:, at] + nh) / ws_ref[:, :1]
            h_ref[:, at] = new
            hs_acc[...] += lane_sum(new)

    def one_sweep(s, carry):
        last = s == sweeps - 1
        ws_half[...] = receive_w(0)
        hs_row[...] = to_row(hs_acc[...])
        hs_acc[...] = jnp.zeros_like(hs_acc)
        sent_nw(0)
        acc_zero(0)

        def step_a(j, carry):
            @pl.when(j == UPDATE_AT)
            def _():
                owner_update(1)

            step(0, j, False)
            return carry

        lax.fori_loop(0, blocks, step_a, 0)
        send_nw(0)
        ws_ref[...] = to_lanes(ws_half[...] + receive_w(1))
        sent_nw(1)
        acc_zero(1)

        def step_b(j, carry):
            @pl.when(j == UPDATE_AT)
            def _():
                owner_update(0)

            step(1, j, last)
            return carry

        lax.fori_loop(0, blocks, step_b, 0)
        send_nw(1)
        return carry

    lax.fori_loop(0, sweeps, one_sweep, 0)
    owner_update(1)
    ws_ref[...] = to_lanes(receive_w(0) + receive_w(1))
    for half in range(2):
        sent_nw(half)
        sent_w(half)


def params():
    return pltpu.CompilerParams(vmem_limit_bytes=VMEM, dimension_semantics=("arbitrary",))


def cost(docs, columns, topics, dots):
    return pl.CostEstimate(flops=int(2 * docs * columns * topics * dots), bytes_accessed=2 * docs * columns, transcendentals=0)


def whole(shape):
    return pl.BlockSpec(shape, lambda j, row: (0,) * len(shape))


def solution(mesh):
    rows, cols = mesh.shape["row"], mesh.shape["col"]

    def body(counts, w_own, h_blk):
        docs, width = counts.shape
        topics = w_own.shape[1]
        mine = width // rows
        blocks = mine // BV
        row = lax.axis_index("row")
        row_arr = row.astype(jnp.int32).reshape(1)
        swap = [(0, 1), (1, 0)]
        sds = jax.ShapeDtypeStruct
        lanes = (topics, 128)

        def total(nw, hs):
            both = jnp.concatenate([nw.reshape(rows * docs, topics), jnp.tile(jnp.sum(hs, axis=1)[None, :], (8, 1))], axis=0)
            both = lax.psum(both, ("row", "col"))
            return both[:rows * docs].reshape(rows, docs, topics), both[rows * docs]

        part = docs // DEVICES
        me = row * cols + lax.axis_index("col")
        vmem, hbm = pl.BlockSpec(memory_space=pltpu.VMEM), pl.BlockSpec(memory_space=pl.ANY)
        dma = pltpu.SemaphoreType.DMA
        V = pltpu.VMEM
        exchange = V((rows, DEVICES, part + EXTRA, topics), F32)
        c_par, h, wb, ws, hs_next, wsl = pl.pallas_call(
            functools.partial(main_kernel, SWEEPS - 3, cols),
            in_specs=[hbm, vmem, hbm],
            out_specs=[hbm] + [vmem] * 5,
            out_shape=[sds((docs, mine), BF16), sds((topics, mine), F32), sds((rows, docs, topics), BF16), sds(lanes, F32),
                       sds(lanes, F32), sds((rows, part, topics), F32)],
            scratch_shapes=[
                V((2, docs, BV), BF16), V((2, topics, BV), F32), V((topics, mine), F32), V((rows, topics, docs), BF16),
                V((2, docs, topics), BF16), V((2, topics, docs), BF16), V((2, EXTRA, topics), F32), V(lanes, F32),
                V(lanes, F32), exchange, exchange, V((rows, DEVICES, EXTRA, topics), F32),
                V((EXTRA, topics), F32), V((EXTRA, topics), F32),
                dma((2,)), dma, dma((2,)), dma, dma((mine // CHUNK,)), dma((mine // CHUNK,)), dma((3,)), dma((3,)),
            ] + [dma((rows, DEVICES))] * 6,
            compiler_params=pltpu.CompilerParams(vmem_limit_bytes=VMEM, collective_id=0, has_side_effects=True),
            cost_estimate=cost(rows * docs, mine, topics, 15), name="main",
        )(counts, w_own, h_blk)
        wbt = jnp.swapaxes(wb, 1, 2)
        ws = ws[:, :1]

        step = 2
        nw_sum = jnp.zeros((rows, docs, topics), F32)
        h_out = jnp.zeros((topics, width), F32)
        for start in range(0, blocks, step):
            with jax.named_scope(f"piece{start}"):
                h_piece, nw, _ = pl.pallas_call(
                    sweep_kernel,
                    grid_spec=pltpu.PrefetchScalarGridSpec(
                        num_scalar_prefetch=1, grid=(step,),
                        in_specs=[
                            pl.BlockSpec((docs, BV), lambda j, row: (0, row[0] * blocks + start + j)),
                            pl.BlockSpec((docs, BV), lambda j, row: (0, start + j)),
                            whole((rows, docs, topics)), whole((rows, topics, docs)), whole((topics, 1)),
                            pl.BlockSpec((topics, BV), lambda j, row: (0, start + j)),
                        ],
                        out_specs=[pl.BlockSpec((topics, BV), lambda j, row: (0, j)), whole((rows, docs, topics)), whole(lanes)]),
                    out_shape=[sds((topics, step * BV), F32), sds((rows, docs, topics), F32), sds(lanes, F32)],
                    compiler_params=params(), cost_estimate=cost(docs, step * BV, topics, 6), name="sweep",
                )(row_arr, counts, c_par, wb, wbt, ws, h)
            nw_sum = nw_sum + nw
            with jax.named_scope(f"send{start}"):
                other = lax.ppermute(h_piece, "row", swap)
            h_out = lax.dynamic_update_slice(h_out, h_piece, (0, row * mine + start * BV))
            h_out = lax.dynamic_update_slice(h_out, other, (0, (1 - row) * mine + start * BV))
        nw, hs = total(nw_sum, hs_next)
        slices = lambda a: lax.dynamic_slice(a, (0, me * part, 0), (rows, part, topics))
        wsl = wsl * slices(nw) / hs[None, None, :]
        w_all = lax.all_gather(wsl, ("row", "col"))
        w_out = lax.dynamic_slice(w_all, (0, row, 0, 0), (DEVICES, 1, part, topics)).reshape(docs, topics)
        return w_out, h_out

    return jax.shard_map(
        body,
        mesh=mesh,
        in_specs=(P(("part", "row"), "col"), P(("part", "row"), None), P("part", "col")),
        out_specs=(P(("part", "row"), None), P("part", "col")),
        check_vma=False,
    )
```

time: 2850 us -> 909 us (0.32)
  waiting for transfers between devices: 2180 us -> 189 us
  Pallas kernels: 0 us -> 661 us
  matrix products: 447 us -> 0 us
  other arithmetic: 122 us -> 5.71 us
  blocking collectives: 48.9 us -> 0 us
    psum x12 -> x1, waiting for transfers between devices: 2180 us -> 70.5 us  [total(): both = lax.psum(both, ('row', 'col'))]
    pallas_call x0 -> x5, Pallas kernels: none -> 661 us  [the longest x1 611 us: body(): pl.pallas_call(functools.partial(main_kernel, SWEEPS - 3, cols), in_specs...]
    dot_general x18 -> x0, matrix products: 447 us -> none  [the longest x6 187 us: local_sweeps(): z_local = jnp.dot(w_bf, h_bf, preferred_element_type=jnp.float32)]
    ppermute x0 -> x4, waiting for transfers between devices: none -> 118 us  [body(): other = lax.ppermute(h_piece, 'row', swap)]
    reduce_sum x12 -> x1, other arithmetic: 102 us -> 0.11 us  [total(): jnp.sum(hs, axis=1)[None, :]]
    psum x7 -> x0, blocking collectives: 48.9 us -> none  [the longest x4 30.1 us: local_sweeps(): w_colsum = lax.psum(w_colsum, 'row')]
    unnamed x4 -> x12, local copies, waits for them, and re-layouts: 34.9 us -> 0.03 us
  transfers between devices with their start and end apart: 12 -> 6, of which waited for: 12 -> 4; matrix products, arithmetic and copies ran while one was open for 8% -> 3% of each run, Pallas kernels for 0% -> 0%
where the time goes in v2:
time: 909 us; the launch traced here: 908 us
  Pallas kernels  661 us (73%)
  waiting for transfers between devices  189 us (21%)
  local copies, waits for them, and re-layouts  34.5 us (4%)
  between operations  14.1 us (2%)
    pallas_call x1, Pallas kernels, body(): pl.pallas_call(functools.partial(main_kernel, SWEEPS - 3, cols), in_specs...  611 us
    ppermute x4, waiting for transfers between devices, body(): other = lax.ppermute(h_piece, 'row', swap)  118 us
    psum x1, waiting for transfers between devices, total(): both = lax.psum(both, ('row', 'col'))  70.5 us
    pallas_call x4, Pallas kernels, body(): pl.pallas_call(sweep_kernel, grid_spec=pltpu.PrefetchScalarGridSpec(num_s...  50.6 us
  transfers between devices with their start and end apart: 6, of which 4 were waited for; matrix products, arithmetic and copies ran while one was open for 3% of the time, Pallas kernels for 0%

profile of v2, /device:TPU:0, one launch (start us, length us, event | category | flops | bytes accessed | tf_op | source)
XLA Modules:
  0.0 907.9 jit_solution(5597370295511205273)
XLA Ops:
  7.2 0.0 all-reduce.2.cloned.1.call-start
  7.2 610.6 %main.1 = (bf16[1024,8192]{1,0:T(8,128)(2,1)}, f32[256,8192]{1,0:T(8,128)}, bf16[2,1024,256]{2,1,0:T(8,128)(2,1)}, f32[256,128]{1,0:T(8,128)}, f32[256,128]{1,0:T(8,128)}, /*index=5*/f32[2,128,256]{2,1,0:T(8,128)}) custom-call(bf16[1024,16384]{1,0:T(8,128)(2,1)} %c_own.7, f32[1024,256]{1,0:T(8,128)} %w_in.1, f32[256,16384]{1,0:T(8,128)} %h_in.1), custom_call_target="tpu_custom_call" | custom-call | flops 128849018880 | bytes 33554432 | tf_op jit(solution)/shard_map/main/pallas_call | solution.py:450
  617.8 2.3 copy.6
  620.1 12.6 %sweep.7 = (f32[256,2048]{1,0:T(8,128)}, f32[2,1024,256]{2,1,0:T(8,128)}, f32[256,128]{1,0:T(8,128)}) custom-call(s32[1]{0:T(128)} %bitcast.row_ref, bf16[1024,16384]{1,0:T(8,128)(2,1)} %c_own.7, bf16[1024,8192]{1,0:T(8,128)(2,1)} %get-tuple-element.17.c_par, bf16[2,1024,256]{2,1,0:T(8,128)(2,1)} %get-tuple-element.18.wb_ref, bf16[2,256,1024]{2,1,0:T(8,128)(2,1)} %bitcast.8, ...), custom_call_target="tpu_custom_call" | custom-call | flops 6442450944 | bytes 4194304 | tf_op jit(solution)/shard_map/piece6/sweep/pallas_call | solution.py:474
  632.7 12.6 %sweep.6 = (f32[256,2048]{1,0:T(8,128)}, f32[2,1024,256]{2,1,0:T(8,128)}, f32[256,128]{1,0:T(8,128)}) custom-call(s32[1]{0:T(128)} %bitcast.row_ref, bf16[1024,16384]{1,0:T(8,128)(2,1)} %c_own.7, bf16[1024,8192]{1,0:T(8,128)(2,1)} %get-tuple-element.17.c_par, bf16[2,1024,256]{2,1,0:T(8,128)(2,1)} %get-tuple-element.18.wb_ref, bf16[2,256,1024]{2,1,0:T(8,128)(2,1)} %bitcast.9, ...), custom_call_target="tpu_custom_call" | custom-call | flops 6442450944 | bytes 4194304 | tf_op jit(solution)/shard_map/piece4/sweep/pallas_call | solution.py:474
  645.2 12.5 %sweep.4 = (f32[256,2048]{1,0:T(8,128)}, f32[2,1024,256]{2,1,0:T(8,128)}, f32[256,128]{1,0:T(8,128)}) custom-call(s32[1]{0:T(128)} %bitcast.row_ref, bf16[1024,16384]{1,0:T(8,128)(2,1)} %c_own.7, bf16[1024,8192]{1,0:T(8,128)(2,1)} %get-tuple-element.17.c_par, bf16[2,1024,256]{2,1,0:T(8,128)(2,1)} %get-tuple-element.18.wb_ref, ...), custom_call_target="tpu_custom_call" | custom-call | flops 6442450944 | bytes 4194304 | tf_op jit(solution)/shard_map/piece0/sweep/pallas_call | solution.py:474
  657.8 0.0 copy-start.5
  657.8 0.0 copy-start
  657.8 12.9 %sweep.5 = (f32[256,2048]{1,0:T(8,128)}, f32[2,1024,256]{2,1,0:T(8,128)}, f32[256,128]{1,0:T(8,128)}) custom-call(s32[1]{0:T(128)} %bitcast.row_ref, bf16[1024,16384]{1,0:T(8,128)(2,1)} %c_own.7, bf16[1024,8192]{1,0:T(8,128)(2,1)} %get-tuple-element.17.c_par, bf16[2,1024,256]{2,1,0:T(8,128)(2,1)} %get-tuple-element.18.wb_ref, ...), custom_call_target="tpu_custom_call" | custom-call | flops 6442450944 | bytes 4194304 | tf_op jit(solution)/shard_map/piece2/sweep/pallas_call | solution.py:474
  670.7 0.0 copy-done.5
  670.7 0.1 reduce_sum.9
  670.8 0.0 copy-done
  670.8 3.4 add_add_fusion
  674.3 0.0 copy-start.4
  674.3 1.5 pad_maximum_fusion
  675.7 0.0 all-reduce.2.cloned.1.call-update
  675.8 0.0 all-gather.3.cloned.1.call-start
  675.8 1.1 collective-permute-start
  676.9 0.0 copy-start.1
  676.9 70.5 %all-reduce.2.cloned.1.call-done = f32[2056,256]{1,0:T(8,128)} async-done(((f32[2056,256]{1,0:T(8,128)}), f32[2056,256]{1,0:T(8,128)}) %all-reduce.2.cloned.1.call-update) | async-done | bytes 2105360 | tf_op jit(solution)/shard_map/psum | solution.py:441
  747.3 0.0 slice-start
  747.3 0.0 slice-start.1
  747.3 0.0 copy-done.4
  747.3 1.6 slice-done
  748.9 0.0 slice-done.1
  748.9 0.7 multiply_divide_fusion
  749.7 0.0 all-gather.3.cloned.1.call-update
  749.7 0.5 collective-permute-start.1
  750.2 1.6 collective-permute-start.2
  751.7 0.0 copy-done.1
  751.7 0.4 collective-permute-start.3
  752.2 8.1 broadcast_in_dim.3
  760.3 3.1 constant_dynamic-update-slice_fusion.7
  763.4 0.0 copy-start.3
  763.4 0.0 collective-permute-done
  763.4 3.3 constant_dynamic-update-slice_fusion.6
  766.7 0.0 copy-done.3
  766.7 1.5 constant_dynamic-update-slice_fusion.5
  768.2 38.5 %collective-permute-done.1 = f32[256,2048]{1,0:T(8,128)} collective-permute-done((f32[256,2048]{1,0:T(8,128)}, f32[256,2048]{1,0:T(8,128)}, u32[]{:S(2)}, u32[]{:S(2)}) %collective-permute-start.1) | collective-permute-done | bytes 2097184 | tf_op jit(solution)/shard_map/send2/ppermute | solution.py:490
  806.6 3.1 constant_dynamic-update-slice_fusion.4
  809.8 0.0 copy-done.2
  809.8 1.5 constant_dynamic-update-slice_fusion.3
  811.2 40.3 %collective-permute-done.2 = f32[256,2048]{1,0:T(8,128)} collective-permute-done((f32[256,2048]{1,0:T(8,128)}, f32[256,2048]{1,0:T(8,128)}, u32[]{:S(2)}, u32[]{:S(2)}) %collective-permute-start.2) | collective-permute-done | bytes 2097184 | tf_op jit(solution)/shard_map/send4/ppermute | solution.py:490
  851.6 3.1 constant_dynamic-update-slice_fusion.2
  854.7 1.5 constant_dynamic-update-slice_fusion.1
  856.2 39.5 %collective-permute-done.3 = f32[256,2048]{1,0:T(8,128)} collective-permute-done((f32[256,2048]{1,0:T(8,128)S(1)}, f32[256,2048]{1,0:T(8,128)}, u32[]{:S(2)}, u32[]{:S(2)}) %collective-permute-start.3) | collective-permute-done | bytes 2097184 | tf_op jit(solution)/shard_map/send6/ppermute | solution.py:490
  895.6 3.1 constant_dynamic-update-slice_fusion
  898.8 2.3 constant_dynamic-slice_fusion
  (3 shorter events, 0.0 us)
Async XLA Ops:
  7.2 740.2 %all-reduce.2.cloned.1.call-start = ((), (), s32[]{:S(2)}) async-start(), calls=%async_computation | async-start | bytes 4210688 | tf_op jit(solution)/shard_map/psum | solution.py:441
  657.8 13.0 %copy-start.5 = (f32[256,128]{1,0:T(8,128)S(1)}, f32[256,128]{1,0:T(8,128)}, u32[]{:S(2)}) copy-start(f32[256,128]{1,0:T(8,128)} %get-tuple-element.25) | copy-start | bytes 393220
  657.8 13.1 %copy-start = (f32[2,1024,256]{2,1,0:T(8,128)S(1)}, f32[2,1024,256]{2,1,0:T(8,128)}, u32[]{:S(2)}) copy-start(f32[2,1024,256]{2,1,0:T(8,128)} %get-tuple-element.24) | copy-start | bytes 6291460
  674.3 73.1 %copy-start.4 = (f32[2,128,256]{2,1,0:T(8,128)S(1)}, f32[2,128,256]{2,1,0:T(8,128)}, u32[]{:S(2)}) copy-start(f32[2,128,256]{2,1,0:T(8,128)} %get-tuple-element.16) | copy-start | bytes 786436
  675.8 223.0 %all-gather.3.cloned.1.call-start = ((), (), s32[]{:S(2)}) async-start(), calls=%async_computation.1 | async-start | bytes 2359296 | tf_op jit(solution)/shard_map/all_gather | solution.py:496
  675.8 87.6 %collective-permute-start = (f32[256,2048]{1,0:T(8,128)}, f32[256,2048]{1,0:T(8,128)}, u32[]{:S(2)}, u32[]{:S(2)}) collective-permute-start(f32[256,2048]{1,0:T(8,128)} %get-tuple-element.26), channel_id=1, source_target_pairs={{0,4},{4,0},{1,5},{5,1},{2,6},{6,2},{3,7},{7,3}} | collective-permute-start | bytes 6291464 | tf_op jit(solution)/shard_map/send0/ppermute | solution.py:490
  676.9 74.9 %copy-start.1 = (f32[256,2048]{1,0:T(8,128)S(1)}, f32[256,2048]{1,0:T(8,128)}, u32[]{:S(2)}) copy-start(f32[256,2048]{1,0:T(8,128)} %get-tuple-element.29) | copy-start | bytes 6291460
  747.3 1.6 slice-start
  747.3 1.6 slice-start.1
  749.7 57.0 %collective-permute-start.1 = (f32[256,2048]{1,0:T(8,128)}, f32[256,2048]{1,0:T(8,128)}, u32[]{:S(2)}, u32[]{:S(2)}) collective-permute-start(f32[256,2048]{1,0:T(8,128)} %get-tuple-element.27), channel_id=1, source_target_pairs={{0,4},{4,0},{1,5},{5,1},{2,6},{6,2},{3,7},{7,3}} | collective-permute-start | bytes 6291464 | tf_op jit(solution)/shard_map/send2/ppermute | solution.py:490
  750.2 101.4 %collective-permute-start.2 = (f32[256,2048]{1,0:T(8,128)}, f32[256,2048]{1,0:T(8,128)}, u32[]{:S(2)}, u32[]{:S(2)}) collective-permute-start(f32[256,2048]{1,0:T(8,128)} %get-tuple-element.28), channel_id=1, source_target_pairs={{0,4},{4,0},{1,5},{5,1},{2,6},{6,2},{3,7},{7,3}} | collective-permute-start | bytes 6291464 | tf_op jit(solution)/shard_map/send4/ppermute | solution.py:490
  751.7 143.9 %collective-permute-start.3 = (f32[256,2048]{1,0:T(8,128)S(1)}, f32[256,2048]{1,0:T(8,128)}, u32[]{:S(2)}, u32[]{:S(2)}) collective-permute-start(f32[256,2048]{1,0:T(8,128)S(1)} %copy-done.1), channel_id=1, source_target_pairs={{0,4},{4,0},{1,5},{5,1},{2,6},{6,2},{3,7},{7,3}} | collective-permute-start | bytes 6291464 | tf_op jit(solution)/shard_map/send6/ppermute | solution.py:490
  763.4 3.3 copy-start.3
  768.2 41.6 %copy-start.2 = (f32[256,2048]{1,0:T(8,128)S(1)}, f32[256,2048]{1,0:T(8,128)}, u32[]{:S(2)}) copy-start(f32[256,2048]{1,0:T(8,128)} %get-tuple-element.28) | copy-start | bytes 6291460
Sparse Core Ops, SparseCore 0:
  675.9 71.4 all-reduce.1
  749.8 30.8 all-gather.2

commit v3 on v2

--- a/solution.py
+++ b/solution.py
@@ -33,41 +33,19 @@
     return out
 
 
-def sweep_body(c_own, c_par, wb_ref, wbt_ref, ws, h, own, par, nw_ref, hs_ref):
-    hb = h.astype(BF16)
-    q_own = ratio(c_own[...], dot(wb_ref[own], hb))
-    nw_ref[own] += dot_t(q_own, hb)
-    nh = dot(wbt_ref[own], q_own)
-    q_par = ratio(c_par[...], dot(wb_ref[par], hb))
-    nw_ref[par] += dot_t(q_par, hb)
-    nh = nh + dot(wbt_ref[par], q_par)
-    new = h * nh / ws
-    hs_ref[...] += lane_sum(new)
-    return new
-
-
-def sweep_kernel(row_ref, c_own, c_par, wb_ref, wbt_ref, ws_ref, h_ref, h_out, nw_ref, hs_ref):
-    own = row_ref[0]
-
-    @pl.when(pl.program_id(0) == 0)
-    def _():
-        nw_ref[...] = jnp.zeros_like(nw_ref)
-        hs_ref[...] = jnp.zeros_like(hs_ref)
-
-    h_out[...] = sweep_body(c_own, c_par, wb_ref, wbt_ref, ws_ref[...], h_ref[...], own, 1 - own, nw_ref, hs_ref)
-
 DEVICES = 8
 EXTRA = 8
 CHUNK = 512
-AHEAD = 6
-UPDATE_AT = 3
+AHEAD = 4
+UPDATE_AT = 4
 
 
 def main_kernel(sweeps, grid_cols, counts, w_in, h_in,
-                c_par, h_ref, wb_ref, ws_ref, hs_acc, wsl_ref,
-                cbuf, hbuf, nh_ref, wbt_ref, wb0, wbt0, ws0_buf, ws0_ref, hs_first, acc, nw_recv, ws_buf, ws_half, hs_row,
+                c_par, h_pair, h_last, w_out,
+                h_ref, wb_ref, ws_ref, hs_acc, wsl_ref, wfin, cbuf, hbuf, nh_ref, wbt_ref, wb0, wbt0, ws0_buf, ws0_ref, hs_first, acc, nw_recv, ws_buf, ws_half, hs_row,
                 csem, psem, hsem, hhsem, c_send, c_got, w0_send, w0_got,
-                nw_send, nw_got, wb_send, wb_got, ws_send, ws_got):
+                nw_send, nw_got, wb_send, wb_got, ws_send, ws_got,
+                h_send, h_got, out_sem, wf_send, wf_got, fin_send, fin_got):
     row, col = lax.axis_index("row"), lax.axis_index("col")
     me = row * grid_cols + col
     docs, full = counts.shape
@@ -96,28 +74,50 @@
     def ws_copy(p, half):
         return remote(ws_buf.at[half, 0], ws_buf.at[half, p], ws_send.at[half, p], ws_got.at[half, p], peer(p)[0])
 
-    def first_copy(q, cross):
-        to_row_, to_col = (1 - row if cross else row), lax.rem(col + q, grid_cols)
-        slot = int(cross)
-        return remote(acc.at[row, to_row_ * grid_cols + to_col], nw_recv.at[row, q], nw_send.at[slot, q],
-                      nw_got.at[row, q], {"row": to_row_, "col": to_col})
-
-    def first_arrival(q, half):
-        return remote(acc.at[0, 0], nw_recv.at[half, q], nw_send.at[0, q], nw_got.at[half, q], partner)
+    def row_peer(q):
+        there = lax.rem(col + q, grid_cols)
+        return {"row": row, "col": there}, there
+
+    def first_copy(q):
+        where, there = row_peer(q)
+        return remote(acc.at[row, pl.ds(2 * there, 2)], nw_recv.at[row, pl.ds(2 * q, 2)], fin_send.at[q], fin_got.at[q], where)
+
+    def first_wb(half, q):
+        where = row_peer(q)[0] if q else partner
+        mine = wb_ref.at[half, pl.ds(pl.multiple_of(col * 2 * part, 2 * part), 2 * part)]
+        return remote(mine, mine, wb_send.at[half, q], wb_got.at[half, q], where)
+
+    def first_ws(half, q):
+        where = row_peer(q)[0] if q else partner
+        return remote(ws_buf.at[half, 0], ws_buf.at[half, q], ws_send.at[half, q], ws_got.at[half, q], where)
+
+    def first_owner(b):
+        d = 2 * col + b
+        return remote(wfin.at[b], wsl_ref.at[row], wf_send.at[b], wf_got.at[row],
+                      {"row": d // grid_cols, "col": lax.rem(d, grid_cols)})
 
     def chunk_copy(j):
         theirs = pl.ds(pl.multiple_of((1 - row) * width + j * CHUNK, CHUNK), CHUNK)
         here = pl.ds(pl.multiple_of(j * CHUNK, CHUNK), CHUNK)
         return remote(counts.at[:, theirs], c_par.at[:, here], c_send.at[j], c_got.at[j], partner)
 
+    half_docs = docs // 2
+
+    def w0_part(of_core):
+        return pl.ds(pl.multiple_of(of_core * half_docs, half_docs), half_docs)
+
+    core = lax.rem(col, 2)
+
     def w0_copies():
-        other = (1 - row) * grid_cols + col
+        at = w0_part(core)
         return [
-            remote(wb0.at[0], wb0.at[1], w0_send.at[0], w0_got.at[0], partner),
+            remote(wb0.at[0, at], wb0.at[1, at], w0_send.at[0], w0_got.at[0], partner),
             remote(ws0_buf.at[0], ws0_buf.at[1], w0_send.at[1], w0_got.at[1], partner),
-            remote(w_in.at[pl.ds(pl.multiple_of(other * part, part), part)], wsl_ref.at[row], w0_send.at[2], w0_got.at[2],
-                   partner),
         ]
+
+    def w0_forward():
+        at = w0_part(core)
+        return remote(wb0.at[1, at], wb0.at[1, at], w0_send.at[2], w0_got.at[2], {"row": row, "col": col + 1 - 2 * core})
 
     def local(src, dst, sem):
         return pltpu.make_async_copy(src, dst, sem)
@@ -148,7 +148,7 @@
 
     def par_chunk(j, slot):
         at = pl.ds(pl.multiple_of(j * CHUNK, CHUNK), CHUNK)
-        return local(c_par.at[:, at], cbuf.at[slot, :, pl.ds(CHUNK, CHUNK)], psem)
+        return local(c_par.at[:, at], cbuf.at[slot, :, pl.ds(CHUNK, CHUNK)], psem.at[slot])
 
     def acc_add(half, res):
         for b in range(DEVICES):
@@ -190,7 +190,6 @@
         total = acc[half, me]
         for p in range(1, DEVICES):
             total = total + nw_recv[half, p]
-        sent_w(half)
         publish(half, total)
 
     def receive_w(half):
@@ -202,6 +201,35 @@
         for p in range(1, DEVICES):
             total = total + ws_buf[half, p]
         return total
+
+    def wfin_copy(half):
+        return remote(wsl_ref.at[half], wfin.at[lax.rem(me, 2)], wf_send.at[half], wf_got.at[lax.rem(me, 2)],
+                      {"row": jnp.int32(half), "col": me // 2})
+
+    def wfin_here(half):
+        return jnp.logical_and(row == half, col == me // 2)
+
+    def fin_copy(q):
+        there = lax.rem(col + q, grid_cols)
+        return remote(acc.at[:, pl.ds(2 * there, 2)], nw_recv.at[:, pl.ds(2 * q, 2)], fin_send.at[q], fin_got.at[q],
+                      {"row": row, "col": there})
+
+    def fin_cross():
+        pair = nw_recv.at[1 - row, pl.ds(0, 2)]
+        return remote(pair, pair, fin_send.at[0], fin_got.at[0], partner)
+
+    def out_copy(q):
+        mine = w_out.at[pl.ds(pl.multiple_of(col * 2 * part, 2 * part), 2 * part)]
+        return remote(mine, mine, fin_send.at[grid_cols + q], fin_got.at[grid_cols + q],
+                      {"row": row, "col": lax.rem(col + q, grid_cols)})
+
+    def h_remote(j):
+        at = pl.ds(pl.multiple_of(j * CHUNK, CHUNK), CHUNK)
+        return remote(h_ref.at[:, at], h_pair.at[row, :, at], h_send.at[j], h_got.at[j], partner)
+
+    def h_local(j):
+        at = pl.ds(pl.multiple_of(j * CHUNK, CHUNK), CHUNK)
+        return local(h_ref.at[:, at], h_pair.at[row, :, at], out_sem.at[j])
 
     def to_row(lanes):
         return jnp.broadcast_to(jnp.sum(lanes.T, axis=0, keepdims=True), (EXTRA, topics))
@@ -218,7 +246,6 @@
     first_c(0, 0).start()
     wb0[0] = w_in[...].astype(BF16)
     ws0_buf[0] = jnp.broadcast_to(jnp.sum(w_in[...], axis=0, keepdims=True), (EXTRA, topics))
-    wsl_ref[row] = w_in[pl.ds(pl.multiple_of(me * part, part), part)]
     pl.semaphore_wait(barrier, DEVICES - 1)
     for copy in w0_copies():
         copy.start()
@@ -272,33 +299,67 @@
 
     hs_row[...] = to_row(hs_first[...])
     acc_sums(row)
-    for q in range(grid_cols):
-        first_copy(q, True).start()
-        if q:
-            first_copy(q, False).start()
+    for q in range(1, grid_cols):
+        first_copy(q).start()
     own_chunk(0, 0).start()
     for copy in w0_copies():
         copy.wait_recv()
+    w0_forward().start()
+    for q in range(1, grid_cols):
+        first_copy(q).wait_recv()
+    total = acc[row, pl.ds(2 * col, 2)]
+    for q in range(1, grid_cols):
+        total = total + nw_recv[row, pl.ds(2 * q, 2)]
+    sums = jnp.zeros((1, topics), F32)
+    for b in range(2):
+        at = pl.ds(pl.multiple_of((2 * col + b) * part, part), part)
+        new = w_in[at] * total[b, :part] / total[b, part:part + 1]
+        wfin[b] = new
+        wb_ref[row, at] = new.astype(BF16)
+        sums = sums + jnp.sum(new, axis=0, keepdims=True)
+    ws_buf[row, 0] = jnp.broadcast_to(sums, (EXTRA, topics))
+    for q in range(grid_cols):
+        first_wb(row, q).start()
+        first_ws(row, q).start()
+    for b in range(2):
+        @pl.when(2 * col + b == me)
+        def _():
+            wsl_ref[row] = wfin[b]
+
+        @pl.when(2 * col + b != me)
+        def _():
+            first_owner(b).start()
+
+    first_wb(1 - row, 0).wait_recv()
+    first_ws(1 - row, 0).wait_recv()
+    for q in range(1, grid_cols):
+        first_wb(1 - row, q).start()
+        first_ws(1 - row, q).start()
+    w0_forward().wait_recv()
     wbt0[1] = wb0[1].T
     ws0_ref[...] = to_lanes(ws0_buf[0] + ws0_buf[1])
     hs_first[...] = jnp.zeros_like(hs_first)
-    total = acc[row, me]
-    for q in range(1, grid_cols):
-        first_arrival(q, row).wait_recv()
-        total = total + nw_recv[row, q]
-    publish(row, total)
-    first_arrival(0, 1 - row).wait_recv()
-    total = nw_recv[1 - row, 0]
-    for q in range(1, grid_cols):
-        first_arrival(q, 1 - row).wait_recv()
-        total = total + nw_recv[1 - row, q]
-    publish(1 - row, total)
-    for q in range(grid_cols):
-        first_copy(q, True).wait_send()
-        if q:
-            first_copy(q, False).wait_send()
+    for q in range(1, grid_cols):
+        first_copy(q).wait_send()
     acc_zero(row)
-    ws_ref[...] = to_lanes(receive_w(0) + receive_w(1))
+    total = ws_buf[0, 0] + ws_buf[1, 0]
+    for half in range(2):
+        for q in range(1, grid_cols):
+            first_wb(half, q).wait_recv()
+            first_ws(half, q).wait_recv()
+            total = total + ws_buf[half, q]
+        wbt_ref[half] = wb_ref[half].T
+    ws_ref[...] = to_lanes(total)
+
+    def both_halves(slot, h):
+        hb = h.astype(BF16)
+        q = ratio(cbuf[slot, :, pl.ds(0, CHUNK)], dot(wb_ref[row], hb))
+        acc_add(row, dot_t(q, hb))
+        nh = dot(wbt_ref[row], q)
+        q = ratio(cbuf[slot, :, pl.ds(CHUNK, CHUNK)], dot(wb_ref[1 - row], hb))
+        acc_add(1 - row, dot_t(q, hb))
+        nh = nh + dot(wbt_ref[1 - row], q)
+        return h * nh / ws_ref[:, :1]
 
     def chunk_step(j, carry):
         slot = lax.rem(j, 2)
@@ -306,7 +367,11 @@
         par_chunk(j, slot).start()
         chunk_copy(j).wait_send()
 
-        @pl.when(jnp.logical_and(j >= AHEAD - 2, j < chunks - 2))
+        @pl.when(j < chunks // 2)
+        def _():
+            chunk_copy(j + AHEAD).start()
+
+        @pl.when(jnp.logical_and(j >= chunks // 2 + AHEAD - 2, j < chunks - 2))
         def _():
             chunk_copy(j + 2).start()
 
@@ -323,14 +388,7 @@
         q = ratio(other, dot(wb0[1], h.astype(BF16)))
         h = h * (nh_ref[:, at] + dot(wbt0[1], q)) / ws0_ref[:, :1]
         hs_first[...] += lane_sum(h)
-        hb = h.astype(BF16)
-        q = ratio(cbuf[slot, :, pl.ds(0, CHUNK)], dot(wb_ref[row], hb))
-        acc_add(row, dot_t(q, hb))
-        nh = dot(wbt_ref[row], q)
-        q = ratio(other, dot(wb_ref[1 - row], hb))
-        acc_add(1 - row, dot_t(q, hb))
-        nh = nh + dot(wbt_ref[1 - row], q)
-        h = h * nh / ws_ref[:, :1]
+        h = both_halves(slot, h)
         h_ref[:, at] = h
         hs_acc[...] += lane_sum(h)
         return carry
@@ -338,6 +396,22 @@
     lax.fori_loop(0, chunks, chunk_step, 0)
     for copy in w0_copies():
         copy.wait_send()
+    w0_forward().wait_send()
+    first_wb(row, 0).wait_send()
+    first_ws(row, 0).wait_send()
+    for half in range(2):
+        for q in range(1, grid_cols):
+            first_wb(half, q).wait_send()
+            first_ws(half, q).wait_send()
+
+        @pl.when(2 * col + half != me)
+        def _():
+            first_owner(half).wait_send()
+
+        @pl.when(jnp.logical_not(wfin_here(half)))
+        def _():
+            remote(wfin.at[0], wsl_ref.at[half], wf_send.at[0], wf_got.at[half], partner).wait_recv()
+
     hs_row[...] = to_row(hs_first[...])
     send_nw(0)
     send_nw(1)
@@ -371,6 +445,7 @@
     def one_sweep(s, carry):
         last = s == sweeps - 1
         ws_half[...] = receive_w(0)
+        sent_w(0)
         hs_row[...] = to_row(hs_acc[...])
         hs_acc[...] = jnp.zeros_like(hs_acc)
         sent_nw(0)
@@ -387,6 +462,7 @@
         lax.fori_loop(0, blocks, step_a, 0)
         send_nw(0)
         ws_ref[...] = to_lanes(ws_half[...] + receive_w(1))
+        sent_w(1)
         sent_nw(1)
         acc_zero(1)
 
@@ -403,23 +479,124 @@
         return carry
 
     lax.fori_loop(0, sweeps, one_sweep, 0)
+    own_chunk(0, 0).start()
+    par_chunk(0, 0).start()
     owner_update(1)
-    ws_ref[...] = to_lanes(receive_w(0) + receive_w(1))
+    for half in range(2):
+        @pl.when(wfin_here(half))
+        def _():
+            wfin[lax.rem(me, 2)] = wsl_ref[half]
+
+        @pl.when(jnp.logical_not(wfin_here(half)))
+        def _():
+            wfin_copy(half).start()
+
+    hs_row[...] = to_row(hs_acc[...])
     for half in range(2):
         sent_nw(half)
+        acc_zero(half)
+    ws_ref[...] = to_lanes(receive_w(0) + receive_w(1))
+
+    def last_step(j, carry):
+        slot = lax.rem(j, 2)
+        own_chunk(j, slot).wait()
+        par_chunk(j, slot).wait()
+
+        @pl.when(j < chunks - 1)
+        def _():
+            own_chunk(j + 1, 1 - slot).start()
+            par_chunk(j + 1, 1 - slot).start()
+
+        @pl.when(j > 0)
+        def _():
+            h_remote(j - 1).start()
+            h_local(j - 1).start()
+
+        at = pl.ds(pl.multiple_of(j * CHUNK, CHUNK), CHUNK)
+        h_ref[:, at] = both_halves(slot, h_ref[:, at])
+        return carry
+
+    lax.fori_loop(0, chunks, last_step, 0)
+    for half in range(2):
+        acc_sums(half)
+    h_local(chunks - 1).start()
+    tail = local(h_ref.at[:, pl.ds(width - CHUNK, CHUNK)], h_last, hhsem)
+    tail.start()
+    for q in range(1, grid_cols):
+        fin_copy(q).start()
+    for half in range(2):
+        @pl.when(jnp.logical_not(wfin_here(half)))
+        def _():
+            wfin_copy(half).wait_send()
+
+    for parity in range(2):
+        @pl.when(2 * col + parity != me)
+        def _():
+            remote(wsl_ref.at[0], wfin.at[parity], wf_send.at[0], wf_got.at[parity], partner).wait_recv()
+
+    for q in range(1, grid_cols):
+        fin_copy(q).wait_recv()
+    ours = acc[row, pl.ds(2 * col, 2)]
+    theirs = acc[1 - row, pl.ds(2 * col, 2)]
+    for q in range(1, grid_cols):
+        ours = ours + nw_recv[row, pl.ds(2 * q, 2)]
+        theirs = theirs + nw_recv[1 - row, pl.ds(2 * q, 2)]
+    nw_recv[1 - row, pl.ds(0, 2)] = theirs
+    fin_cross().start()
+    fin_cross().wait_recv()
+    total = ours + nw_recv[row, pl.ds(0, 2)]
+    new = wfin[...] * total[:, :part] / total[:1, part:part + 1]
+    for b in range(2):
+        w_out[pl.ds(pl.multiple_of((2 * col + b) * part, part), part)] = new[b]
+    for q in range(1, grid_cols):
+        out_copy(q).start()
+    for half in range(2):
         sent_w(half)
-
-
-def params():
-    return pltpu.CompilerParams(vmem_limit_bytes=VMEM, dimension_semantics=("arbitrary",))
+    for q in range(1, grid_cols):
+        out_copy(q).wait()
+        fin_copy(q).wait_send()
+    fin_cross().wait_send()
+
+    tail.wait()
+
+    def drain(j, carry):
+        h_remote(j).wait_recv()
+        h_remote(j).wait_send()
+        h_local(j).wait()
+        return carry
+
+    lax.fori_loop(0, chunks - 1, drain, 0)
+    h_local(chunks - 1).wait()
+
+
+PLACE = 2048
+
+
+def place_kernel(h_pair, h_out, buf, in_sem, out_sem):
+    row = lax.axis_index("row")
+    width = h_pair.shape[2]
+    jobs = []
+    for other in range(2):
+        half = 1 - row if other else row
+        for start in range(0, width, PLACE):
+            size = PLACE - CHUNK if other and start + PLACE == width else PLACE
+            n = len(jobs)
+            held = buf.at[n, :, pl.ds(0, size)]
+            jobs.append((
+                pltpu.make_async_copy(h_pair.at[half, :, pl.ds(start, size)], held, in_sem.at[n]),
+                pltpu.make_async_copy(held, h_out.at[:, pl.ds(pl.multiple_of(half * width + start, PLACE), size)], out_sem.at[n]),
+            ))
+    for load, _ in jobs:
+        load.start()
+    for load, store in jobs:
+        load.wait()
+        store.start()
+    for _, store in jobs:
+        store.wait()
 
 
 def cost(docs, columns, topics, dots):
     return pl.CostEstimate(flops=int(2 * docs * columns * topics * dots), bytes_accessed=2 * docs * columns, transcendentals=0)
-
-
-def whole(shape):
-    return pl.BlockSpec(shape, lambda j, row: (0,) * len(shape))
 
 
 def solution(mesh):
@@ -429,72 +606,43 @@
         docs, width = counts.shape
         topics = w_own.shape[1]
         mine = width // rows
-        blocks = mine // BV
-        row = lax.axis_index("row")
-        row_arr = row.astype(jnp.int32).reshape(1)
-        swap = [(0, 1), (1, 0)]
         sds = jax.ShapeDtypeStruct
         lanes = (topics, 128)
-
-        def total(nw, hs):
-            both = jnp.concatenate([nw.reshape(rows * docs, topics), jnp.tile(jnp.sum(hs, axis=1)[None, :], (8, 1))], axis=0)
-            both = lax.psum(both, ("row", "col"))
-            return both[:rows * docs].reshape(rows, docs, topics), both[rows * docs]
-
         part = docs // DEVICES
-        me = row * cols + lax.axis_index("col")
         vmem, hbm = pl.BlockSpec(memory_space=pltpu.VMEM), pl.BlockSpec(memory_space=pl.ANY)
         dma = pltpu.SemaphoreType.DMA
         V = pltpu.VMEM
         exchange = V((rows, DEVICES, part + EXTRA, topics), F32)
-        c_par, h, wb, ws, hs_next, wsl = pl.pallas_call(
+        pieces = mine // CHUNK
+        c_par, h_pair, h_last, w_out = pl.pallas_call(
             functools.partial(main_kernel, SWEEPS - 3, cols),
             in_specs=[hbm, vmem, hbm],
-            out_specs=[hbm] + [vmem] * 5,
-            out_shape=[sds((docs, mine), BF16), sds((topics, mine), F32), sds((rows, docs, topics), BF16), sds(lanes, F32),
-                       sds(lanes, F32), sds((rows, part, topics), F32)],
+            out_specs=[hbm, hbm, hbm, vmem],
+            out_shape=[sds((docs, mine), BF16), sds((rows, topics, mine), F32), sds((topics, CHUNK), F32),
+                       sds((docs, topics), F32)],
             scratch_shapes=[
+                V((topics, mine), F32), V((rows, docs, topics), BF16), V(lanes, F32), V(lanes, F32),
+                V((rows, part, topics), F32), V((2, part, topics), F32),
                 V((2, docs, BV), BF16), V((2, topics, BV), F32), V((topics, mine), F32), V((rows, topics, docs), BF16),
                 V((2, docs, topics), BF16), V((2, topics, docs), BF16), V((2, EXTRA, topics), F32), V(lanes, F32),
                 V(lanes, F32), exchange, exchange, V((rows, DEVICES, EXTRA, topics), F32),
                 V((EXTRA, topics), F32), V((EXTRA, topics), F32),
-                dma((2,)), dma, dma((2,)), dma, dma((mine // CHUNK,)), dma((mine // CHUNK,)), dma((3,)), dma((3,)),
-            ] + [dma((rows, DEVICES))] * 6,
+                dma((2,)), dma((2,)), dma((2,)), dma, dma((pieces,)), dma((pieces,)), dma((3,)), dma((3,)),
+            ] + [dma((rows, DEVICES))] * 6 + [dma((pieces,))] * 3 + [dma((2,))] * 2 + [dma((2 * cols,))] * 2,
             compiler_params=pltpu.CompilerParams(vmem_limit_bytes=VMEM, collective_id=0, has_side_effects=True),
-            cost_estimate=cost(rows * docs, mine, topics, 15), name="main",
+            cost_estimate=cost(rows * docs, mine, topics, 18), name="main",
         )(counts, w_own, h_blk)
-        wbt = jnp.swapaxes(wb, 1, 2)
-        ws = ws[:, :1]
-
-        step = 2
-        nw_sum = jnp.zeros((rows, docs, topics), F32)
-        h_out = jnp.zeros((topics, width), F32)
-        for start in range(0, blocks, step):
-            with jax.named_scope(f"piece{start}"):
-                h_piece, nw, _ = pl.pallas_call(
-                    sweep_kernel,
-                    grid_spec=pltpu.PrefetchScalarGridSpec(
-                        num_scalar_prefetch=1, grid=(step,),
-                        in_specs=[
-                            pl.BlockSpec((docs, BV), lambda j, row: (0, row[0] * blocks + start + j)),
-                            pl.BlockSpec((docs, BV), lambda j, row: (0, start + j)),
-                            whole((rows, docs, topics)), whole((rows, topics, docs)), whole((topics, 1)),
-                            pl.BlockSpec((topics, BV), lambda j, row: (0, start + j)),
-                        ],
-                        out_specs=[pl.BlockSpec((topics, BV), lambda j, row: (0, j)), whole((rows, docs, topics)), whole(lanes)]),
-                    out_shape=[sds((topics, step * BV), F32), sds((rows, docs, topics), F32), sds(lanes, F32)],
-                    compiler_params=params(), cost_estimate=cost(docs, step * BV, topics, 6), name="sweep",
-                )(row_arr, counts, c_par, wb, wbt, ws, h)
-            nw_sum = nw_sum + nw
-            with jax.named_scope(f"send{start}"):
-                other = lax.ppermute(h_piece, "row", swap)
-            h_out = lax.dynamic_update_slice(h_out, h_piece, (0, row * mine + start * BV))
-            h_out = lax.dynamic_update_slice(h_out, other, (0, (1 - row) * mine + start * BV))
-        nw, hs = total(nw_sum, hs_next)
-        slices = lambda a: lax.dynamic_slice(a, (0, me * part, 0), (rows, part, topics))
-        wsl = wsl * slices(nw) / hs[None, None, :]
-        w_all = lax.all_gather(wsl, ("row", "col"))
-        w_out = lax.dynamic_slice(w_all, (0, row, 0, 0), (DEVICES, 1, part, topics)).reshape(docs, topics)
+        other = lax.ppermute(h_last, "row", [(0, 1), (1, 0)])
+        row = lax.axis_index("row")
+        jobs = 2 * mine // PLACE
+        h_out = pl.pallas_call(
+            place_kernel,
+            in_specs=[hbm], out_specs=hbm, out_shape=sds((topics, width), F32),
+            scratch_shapes=[V((jobs, topics, PLACE), F32), dma((jobs,)), dma((jobs,))],
+            compiler_params=pltpu.CompilerParams(vmem_limit_bytes=VMEM),
+            cost_estimate=pl.CostEstimate(flops=10 ** 8, bytes_accessed=8 * topics * width, transcendentals=0), name="place",
+        )(h_pair)
+        h_out = lax.dynamic_update_slice(h_out, other, (0, (1 - row) * mine + mine - CHUNK))
         return w_out, h_out
 
     return jax.shard_map(

time: 909 us -> 771 us (0.85)
  waiting for transfers between devices: 189 us -> 0.63 us
  Pallas kernels: 661 us -> 763 us
  local copies, waits for them, and re-layouts: 34.5 us -> 1.8 us
  between operations: 14.1 us -> 0.65 us
    pallas_call x1, Pallas kernels: 611 us -> 751 us  [body(): pl.pallas_call(functools.partial(main_kernel, SWEEPS - 3, cols), in_specs...]
    ppermute x4 -> x1, waiting for transfers between devices: 118 us -> 0.63 us  [body(): other = lax.ppermute(h_last, 'row', [(0, 1), (1, 0)])]
    psum x1 -> x0, waiting for transfers between devices: 70.5 us -> none  [total(): both = lax.psum(both, ('row', 'col'))]
    pallas_call x4 -> x1, Pallas kernels: 50.6 us -> 11.7 us  [body(): pl.pallas_call(place_kernel, in_specs=[hbm], out_specs=hbm, out_shape=sds...]
    dynamic_update_slice x8 -> x1, local copies, waits for them, and re-layouts: 20.2 us -> 0.83 us  [body(): lax.dynamic_update_slice(h_out, other, (0, (1 - row) * mine + mine - CHUNK))]
  transfers between devices with their start and end apart: 6 -> 1, of which waited for: 4 -> 1; matrix products, arithmetic and copies ran while one was open for 3% -> 0% of each run, Pallas kernels for 0% -> 2%
where the time goes in v3:
time: 771 us; the launch traced here: 770 us
  Pallas kernels  763 us (99%)
    pallas_call x1, Pallas kernels, body(): pl.pallas_call(functools.partial(main_kernel, SWEEPS - 3, cols), in_specs...  751 us
  transfers between devices with their start and end apart: 1, of which 1 were waited for; matrix products, arithmetic and copies ran while one was open for 0% of the time, Pallas kernels for 2%

profile of v3, /device:TPU:0, one launch (start us, length us, event | category | flops | bytes accessed | tf_op | source)
XLA Modules:
  0.0 770.4 jit_solution(5037866586614962621)
XLA Ops:
  0.6 751.3 %main.1 = (bf16[1024,8192]{1,0:T(8,128)(2,1)}, f32[2,256,8192]{2,1,0:T(8,128)}, f32[256,512]{1,0:T(8,128)}, f32[1024,256]{1,0:T(8,128)}) custom-call(bf16[1024,16384]{1,0:T(8,128)(2,1)} %counts.1, f32[1024,256]{1,0:T(8,128)} %w_in.1, f32[256,16384]{1,0:T(8,128)} %h_in.1), custom_call_target="tpu_custom_call" | custom-call | flops 154618822656 | bytes 33554432 | tf_op jit(solution)/shard_map/main/pallas_call | solution.py:617
  751.9 4.4 collective-permute-start
  756.2 0.0 copy-start
  756.3 11.7 %place.1 = f32[256,16384]{1,0:T(8,128)} custom-call(f32[2,256,8192]{2,1,0:T(8,128)} %get-tuple-element.6.h_pair), custom_call_target="tpu_custom_call" | custom-call | flops 100000000 | bytes 33554432 | tf_op jit(solution)/shard_map/place/pallas_call | solution.py:638
  768.0 0.6 collective-permute-done
  768.6 0.8 constant_dynamic-update-slice_fusion
  769.4 0.0 copy-done
  769.4 1.0 copy.7
Async XLA Ops:
  751.9 16.7 %collective-permute-start = (f32[256,512]{1,0:T(8,128)}, f32[256,512]{1,0:T(8,128)S(1)}, u32[]{:S(2)}, u32[]{:S(2)}) collective-permute-start(f32[256,512]{1,0:T(8,128)} %get-tuple-element.7), channel_id=1, source_target_pairs={{0,4},{4,0},{1,5},{5,1},{2,6},{6,2},{3,7},{7,3}} | collective-permute-start | bytes 1572872 | tf_op jit(solution)/shard_map/ppermute | solution.py:635
  756.2 13.2 %copy-start = (f32[1024,256]{1,0:T(8,128)S(1)}, f32[1024,256]{1,0:T(8,128)}, u32[]{:S(2)}) copy-start(f32[1024,256]{1,0:T(8,128)} %get-tuple-element.10) | copy-start | bytes 3145732

commit v4 on v3

--- a/solution.py
+++ b/solution.py
@@ -34,10 +34,12 @@
 
 
 DEVICES = 8
+CHIPS = 4
 EXTRA = 8
 CHUNK = 512
 AHEAD = 4
-UPDATE_AT = 4
+UPDATE_AT = 5
+RELAY_AT = 0
 
 
 def main_kernel(sweeps, grid_cols, counts, w_in, h_in,
@@ -45,7 +47,7 @@
                 h_ref, wb_ref, ws_ref, hs_acc, wsl_ref, wfin, cbuf, hbuf, nh_ref, wbt_ref, wb0, wbt0, ws0_buf, ws0_ref, hs_first, acc, nw_recv, ws_buf, ws_half, hs_row,
                 csem, psem, hsem, hhsem, c_send, c_got, w0_send, w0_got,
                 nw_send, nw_got, wb_send, wb_got, ws_send, ws_got,
-                h_send, h_got, out_sem, wf_send, wf_got, fin_send, fin_got):
+                mate_recv, mate_send, mate_got, h_send, h_got, out_sem, wf_send, wf_got, fin_send, fin_got):
     row, col = lax.axis_index("row"), lax.axis_index("col")
     me = row * grid_cols + col
     docs, full = counts.shape
@@ -63,9 +65,17 @@
         other = lax.rem(me + p, DEVICES)
         return {"row": other // grid_cols, "col": lax.rem(other, grid_cols)}, other
 
+    core, chip = lax.rem(col, 2), me // 2
+    mate = {"row": row, "col": col + 1 - 2 * core}
+
+    def mate_copy(half):
+        return remote(acc.at[half, 1 - core], mate_recv.at[half], mate_send.at[half], mate_got.at[half], mate)
+
     def nw_copy(p, half):
-        where, other = peer(p)
-        return remote(acc.at[half, other], nw_recv.at[half, p], nw_send.at[half, p], nw_got.at[half, p], where)
+        there = lax.rem(chip + p, CHIPS)
+        d = 2 * there + core
+        return remote(acc.at[half, core, there], nw_recv.at[half, p], nw_send.at[half, p], nw_got.at[half, p],
+                      {"row": d // grid_cols, "col": lax.rem(d, grid_cols)})
 
     def wb_copy(p, half):
         mine = wb_ref.at[half, pl.ds(pl.multiple_of(me * part, part), part)]
@@ -80,7 +90,7 @@
 
     def first_copy(q):
         where, there = row_peer(q)
-        return remote(acc.at[row, pl.ds(2 * there, 2)], nw_recv.at[row, pl.ds(2 * q, 2)], fin_send.at[q], fin_got.at[q], where)
+        return remote(acc.at[row, :, there], nw_recv.at[row, pl.ds(2 * q, 2)], fin_send.at[q], fin_got.at[q], where)
 
     def first_wb(half, q):
         where = row_peer(q)[0] if q else partner
@@ -105,8 +115,6 @@
 
     def w0_part(of_core):
         return pl.ds(pl.multiple_of(of_core * half_docs, half_docs), half_docs)
-
-    core = lax.rem(col, 2)
 
     def w0_copies():
         at = w0_part(core)
@@ -117,7 +125,7 @@
 
     def w0_forward():
         at = w0_part(core)
-        return remote(wb0.at[1, at], wb0.at[1, at], w0_send.at[2], w0_got.at[2], {"row": row, "col": col + 1 - 2 * core})
+        return remote(wb0.at[1, at], wb0.at[1, at], w0_send.at[2], w0_got.at[2], mate)
 
     def local(src, dst, sem):
         return pltpu.make_async_copy(src, dst, sem)
@@ -152,18 +160,23 @@
 
     def acc_add(half, res):
         for b in range(DEVICES):
-            acc[half, b, pl.ds(0, part)] += res[b * part:(b + 1) * part]
+            acc[half, b % 2, b // 2, pl.ds(0, part)] += res[b * part:(b + 1) * part]
 
     def acc_sums(half):
         for b in range(DEVICES):
-            acc[half, b, pl.ds(part, EXTRA)] = hs_row[...]
+            acc[half, b % 2, b // 2, pl.ds(part, EXTRA)] = hs_row[...]
 
     def acc_zero(half):
         acc[half] = jnp.zeros(acc.shape[1:], F32)
 
     def send_nw(half):
         acc_sums(half)
-        for p in range(1, DEVICES):
+        mate_copy(half).start()
+
+    def relay(half):
+        mate_copy(half).wait_recv()
+        acc[half, core] += mate_recv[half]
+        for p in range(1, CHIPS):
             nw_copy(p, half).start()
 
     def publish(half, total):
@@ -181,14 +194,15 @@
             ws_copy(p, half).wait_send()
 
     def sent_nw(half):
-        for p in range(1, DEVICES):
+        mate_copy(half).wait_send()
+        for p in range(1, CHIPS):
             nw_copy(p, half).wait_send()
 
     def owner_update(half):
-        for p in range(1, DEVICES):
+        for p in range(1, CHIPS):
             nw_copy(p, half).wait_recv()
-        total = acc[half, me]
-        for p in range(1, DEVICES):
+        total = acc[half, core, chip]
+        for p in range(1, CHIPS):
             total = total + nw_recv[half, p]
         publish(half, total)
 
@@ -211,7 +225,7 @@
 
     def fin_copy(q):
         there = lax.rem(col + q, grid_cols)
-        return remote(acc.at[:, pl.ds(2 * there, 2)], nw_recv.at[:, pl.ds(2 * q, 2)], fin_send.at[q], fin_got.at[q],
+        return remote(acc.at[:, :, there], nw_recv.at[:, pl.ds(2 * q, 2)], fin_send.at[q], fin_got.at[q],
                       {"row": row, "col": there})
 
     def fin_cross():
@@ -307,7 +321,7 @@
     w0_forward().start()
     for q in range(1, grid_cols):
         first_copy(q).wait_recv()
-    total = acc[row, pl.ds(2 * col, 2)]
+    total = acc[row, :, col]
     for q in range(1, grid_cols):
         total = total + nw_recv[row, pl.ds(2 * q, 2)]
     sums = jnp.zeros((1, topics), F32)
@@ -416,6 +430,7 @@
     send_nw(0)
     send_nw(1)
     c_start(0, 0, 0)
+    relay(0)
     owner_update(0)
 
     def step(half, j, last):
@@ -452,6 +467,10 @@
         acc_zero(0)
 
         def step_a(j, carry):
+            @pl.when(j == RELAY_AT)
+            def _():
+                relay(1)
+
             @pl.when(j == UPDATE_AT)
             def _():
                 owner_update(1)
@@ -467,6 +486,10 @@
         acc_zero(1)
 
         def step_b(j, carry):
+            @pl.when(j == RELAY_AT)
+            def _():
+                relay(0)
+
             @pl.when(j == UPDATE_AT)
             def _():
                 owner_update(0)
@@ -481,6 +504,7 @@
     lax.fori_loop(0, sweeps, one_sweep, 0)
     own_chunk(0, 0).start()
     par_chunk(0, 0).start()
+    relay(1)
     owner_update(1)
     for half in range(2):
         @pl.when(wfin_here(half))
@@ -536,8 +560,8 @@
 
     for q in range(1, grid_cols):
         fin_copy(q).wait_recv()
-    ours = acc[row, pl.ds(2 * col, 2)]
-    theirs = acc[1 - row, pl.ds(2 * col, 2)]
+    ours = acc[row, :, col]
+    theirs = acc[1 - row, :, col]
     for q in range(1, grid_cols):
         ours = ours + nw_recv[row, pl.ds(2 * q, 2)]
         theirs = theirs + nw_recv[1 - row, pl.ds(2 * q, 2)]
@@ -613,6 +637,7 @@
         dma = pltpu.SemaphoreType.DMA
         V = pltpu.VMEM
         exchange = V((rows, DEVICES, part + EXTRA, topics), F32)
+        partial = V((rows, 2, CHIPS, part + EXTRA, topics), F32)
         pieces = mine // CHUNK
         c_par, h_pair, h_last, w_out = pl.pallas_call(
             functools.partial(main_kernel, SWEEPS - 3, cols),
@@ -625,10 +650,10 @@
                 V((rows, part, topics), F32), V((2, part, topics), F32),
                 V((2, docs, BV), BF16), V((2, topics, BV), F32), V((topics, mine), F32), V((rows, topics, docs), BF16),
                 V((2, docs, topics), BF16), V((2, topics, docs), BF16), V((2, EXTRA, topics), F32), V(lanes, F32),
-                V(lanes, F32), exchange, exchange, V((rows, DEVICES, EXTRA, topics), F32),
+                V(lanes, F32), partial, exchange, V((rows, DEVICES, EXTRA, topics), F32),
                 V((EXTRA, topics), F32), V((EXTRA, topics), F32),
                 dma((2,)), dma((2,)), dma((2,)), dma, dma((pieces,)), dma((pieces,)), dma((3,)), dma((3,)),
-            ] + [dma((rows, DEVICES))] * 6 + [dma((pieces,))] * 3 + [dma((2,))] * 2 + [dma((2 * cols,))] * 2,
+            ] + [dma((rows, DEVICES))] * 6 + [V((rows, CHIPS, part + EXTRA, topics), F32), dma((rows,)), dma((rows,))] + [dma((pieces,))] * 3 + [dma((2,))] * 2 + [dma((2 * cols,))] * 2,
             compiler_params=pltpu.CompilerParams(vmem_limit_bytes=VMEM, collective_id=0, has_side_effects=True),
             cost_estimate=cost(rows * docs, mine, topics, 18), name="main",
         )(counts, w_own, h_blk)

time: 771 us -> 738 us (0.957)
  Pallas kernels: 763 us -> 731 us
    pallas_call x1, Pallas kernels: 751 us -> 719 us  [body(): pl.pallas_call(functools.partial(main_kernel, SWEEPS - 3, cols), in_specs...]
where the time goes in v4:
time: 738 us
  Pallas kernels  731 us (99%)
    pallas_call x1, Pallas kernels, body(): pl.pallas_call(functools.partial(main_kernel, SWEEPS - 3, cols), in_specs...  719 us
  transfers between devices with their start and end apart: 1, of which 1 were waited for; matrix products, arithmetic and copies ran while one was open for 0% of the time, Pallas kernels for 2%

profile of v4, /device:TPU:0, one launch (start us, length us, event | category | flops | bytes accessed | tf_op | source)
XLA Modules:
  0.0 737.7 jit_solution(16402767308269591232)
XLA Ops:
  0.6 719.3 %main.1 = (bf16[1024,8192]{1,0:T(8,128)(2,1)}, f32[2,256,8192]{2,1,0:T(8,128)}, f32[256,512]{1,0:T(8,128)}, f32[1024,256]{1,0:T(8,128)}) custom-call(bf16[1024,16384]{1,0:T(8,128)(2,1)} %counts.1, f32[1024,256]{1,0:T(8,128)} %w_in.1, f32[256,16384]{1,0:T(8,128)} %h_in.1), custom_call_target="tpu_custom_call" | custom-call | flops 154618822656 | bytes 33554432 | tf_op jit(solution)/shard_map/main/pallas_call | solution.py:642
  719.9 3.2 collective-permute-start
  723.2 0.0 copy-start
  723.2 11.7 %place.1 = f32[256,16384]{1,0:T(8,128)} custom-call(f32[2,256,8192]{2,1,0:T(8,128)} %get-tuple-element.6.h_pair), custom_call_target="tpu_custom_call" | custom-call | flops 100000000 | bytes 33554432 | tf_op jit(solution)/shard_map/place/pallas_call | solution.py:663
  734.9 1.0 collective-permute-done
  735.9 0.8 constant_dynamic-update-slice_fusion
  736.7 0.0 copy-done
  736.7 1.0 copy.7
Async XLA Ops:
  719.9 15.9 %collective-permute-start = (f32[256,512]{1,0:T(8,128)}, f32[256,512]{1,0:T(8,128)S(1)}, u32[]{:S(2)}, u32[]{:S(2)}) collective-permute-start(f32[256,512]{1,0:T(8,128)} %get-tuple-element.7), channel_id=1, source_target_pairs={{0,4},{4,0},{1,5},{5,1},{2,6},{6,2},{3,7},{7,3}} | collective-permute-start | bytes 1572872 | tf_op jit(solution)/shard_map/ppermute | solution.py:660
  723.2 13.5 %copy-start = (f32[1024,256]{1,0:T(8,128)S(1)}, f32[1024,256]{1,0:T(8,128)}, u32[]{:S(2)}) copy-start(f32[1024,256]{1,0:T(8,128)} %get-tuple-element.10) | copy-start | bytes 3145732

commit v5 on v4

--- a/solution.py
+++ b/solution.py
@@ -37,7 +37,8 @@
 CHIPS = 4
 EXTRA = 8
 CHUNK = 512
-AHEAD = 4
+ARRIVE = 256
+AHEAD = 8
 UPDATE_AT = 5
 RELAY_AT = 0
 
@@ -54,6 +55,7 @@
     topics, width = h_ref.shape
     blocks = width // BV
     chunks = width // CHUNK
+    arrivals = width // ARRIVE
     part = docs // DEVICES
     partner = {"row": 1 - row, "col": col}
     mesh_id = pl.DeviceIdType.MESH
@@ -107,25 +109,20 @@
                       {"row": d // grid_cols, "col": lax.rem(d, grid_cols)})
 
     def chunk_copy(j):
-        theirs = pl.ds(pl.multiple_of((1 - row) * width + j * CHUNK, CHUNK), CHUNK)
-        here = pl.ds(pl.multiple_of(j * CHUNK, CHUNK), CHUNK)
+        theirs = pl.ds(pl.multiple_of((1 - row) * width + j * ARRIVE, ARRIVE), ARRIVE)
+        here = pl.ds(pl.multiple_of(j * ARRIVE, ARRIVE), ARRIVE)
         return remote(counts.at[:, theirs], c_par.at[:, here], c_send.at[j], c_got.at[j], partner)
 
-    half_docs = docs // 2
-
-    def w0_part(of_core):
-        return pl.ds(pl.multiple_of(of_core * half_docs, half_docs), half_docs)
-
     def w0_copies():
-        at = w0_part(core)
+        at = pl.ds(pl.multiple_of(col * 2 * part, 2 * part), 2 * part)
         return [
             remote(wb0.at[0, at], wb0.at[1, at], w0_send.at[0], w0_got.at[0], partner),
-            remote(ws0_buf.at[0], ws0_buf.at[1], w0_send.at[1], w0_got.at[1], partner),
+            remote(ws0_buf.at[0], ws0_buf.at[1], w0_send.at[grid_cols], w0_got.at[grid_cols], partner),
         ]
 
-    def w0_forward():
-        at = w0_part(core)
-        return remote(wb0.at[1, at], wb0.at[1, at], w0_send.at[2], w0_got.at[2], mate)
+    def w0_forward(q):
+        at = pl.ds(pl.multiple_of(col * 2 * part, 2 * part), 2 * part)
+        return remote(wb0.at[1, at], wb0.at[1, at], w0_send.at[q], w0_got.at[q], row_peer(q)[0])
 
     def local(src, dst, sem):
         return pltpu.make_async_copy(src, dst, sem)
@@ -150,13 +147,13 @@
         at = pl.ds(pl.multiple_of((1 - row) * width + j * BV, BV), BV)
         return local(h_in.at[:, at], hbuf.at[slot], hsem.at[slot])
 
-    def own_chunk(j, slot):
-        at = pl.ds(pl.multiple_of(row * width + j * CHUNK, CHUNK), CHUNK)
-        return local(counts.at[:, at], cbuf.at[slot, :, pl.ds(0, CHUNK)], csem.at[slot])
-
-    def par_chunk(j, slot):
-        at = pl.ds(pl.multiple_of(j * CHUNK, CHUNK), CHUNK)
-        return local(c_par.at[:, at], cbuf.at[slot, :, pl.ds(CHUNK, CHUNK)], psem.at[slot])
+    def own_chunk(j, slot, size=CHUNK):
+        at = pl.ds(pl.multiple_of(row * width + j * size, size), size)
+        return local(counts.at[:, at], cbuf.at[slot, :, pl.ds(0, size)], csem.at[slot])
+
+    def par_chunk(j, slot, size=CHUNK):
+        at = pl.ds(pl.multiple_of(j * size, size), size)
+        return local(c_par.at[:, at], cbuf.at[slot, :, pl.ds(CHUNK, size)], psem.at[slot])
 
     def acc_add(half, res):
         for b in range(DEVICES):
@@ -315,10 +312,11 @@
     acc_sums(row)
     for q in range(1, grid_cols):
         first_copy(q).start()
-    own_chunk(0, 0).start()
+    own_chunk(0, 0, ARRIVE).start()
     for copy in w0_copies():
         copy.wait_recv()
-    w0_forward().start()
+    for q in range(1, grid_cols):
+        w0_forward(q).start()
     for q in range(1, grid_cols):
         first_copy(q).wait_recv()
     total = acc[row, :, col]
@@ -349,7 +347,8 @@
     for q in range(1, grid_cols):
         first_wb(1 - row, q).start()
         first_ws(1 - row, q).start()
-    w0_forward().wait_recv()
+    for q in range(1, grid_cols):
+        w0_forward(q).wait_recv()
     wbt0[1] = wb0[1].T
     ws0_ref[...] = to_lanes(ws0_buf[0] + ws0_buf[1])
     hs_first[...] = jnp.zeros_like(hs_first)
@@ -366,11 +365,12 @@
     ws_ref[...] = to_lanes(total)
 
     def both_halves(slot, h):
+        size = h.shape[1]
         hb = h.astype(BF16)
-        q = ratio(cbuf[slot, :, pl.ds(0, CHUNK)], dot(wb_ref[row], hb))
+        q = ratio(cbuf[slot, :, pl.ds(0, size)], dot(wb_ref[row], hb))
         acc_add(row, dot_t(q, hb))
         nh = dot(wbt_ref[row], q)
-        q = ratio(cbuf[slot, :, pl.ds(CHUNK, CHUNK)], dot(wb_ref[1 - row], hb))
+        q = ratio(cbuf[slot, :, pl.ds(CHUNK, size)], dot(wb_ref[1 - row], hb))
         acc_add(1 - row, dot_t(q, hb))
         nh = nh + dot(wbt_ref[1 - row], q)
         return h * nh / ws_ref[:, :1]
@@ -378,27 +378,27 @@
     def chunk_step(j, carry):
         slot = lax.rem(j, 2)
         chunk_copy(j).wait_recv()
-        par_chunk(j, slot).start()
+        par_chunk(j, slot, ARRIVE).start()
         chunk_copy(j).wait_send()
 
-        @pl.when(j < chunks // 2)
+        @pl.when(j < arrivals // 2)
         def _():
             chunk_copy(j + AHEAD).start()
 
-        @pl.when(jnp.logical_and(j >= chunks // 2 + AHEAD - 2, j < chunks - 2))
+        @pl.when(jnp.logical_and(j >= arrivals // 2 + AHEAD - 2, j < arrivals - 2))
         def _():
             chunk_copy(j + 2).start()
 
-        own_chunk(j, slot).wait()
-
-        @pl.when(j < chunks - 1)
-        def _():
-            own_chunk(j + 1, 1 - slot).start()
-
-        at = pl.ds(pl.multiple_of(j * CHUNK, CHUNK), CHUNK)
+        own_chunk(j, slot, ARRIVE).wait()
+
+        @pl.when(j < arrivals - 1)
+        def _():
+            own_chunk(j + 1, 1 - slot, ARRIVE).start()
+
+        at = pl.ds(pl.multiple_of(j * ARRIVE, ARRIVE), ARRIVE)
         h = h_ref[:, at]
-        par_chunk(j, slot).wait()
-        other = cbuf[slot, :, pl.ds(CHUNK, CHUNK)]
+        par_chunk(j, slot, ARRIVE).wait()
+        other = cbuf[slot, :, pl.ds(CHUNK, ARRIVE)]
         q = ratio(other, dot(wb0[1], h.astype(BF16)))
         h = h * (nh_ref[:, at] + dot(wbt0[1], q)) / ws0_ref[:, :1]
         hs_first[...] += lane_sum(h)
@@ -407,10 +407,11 @@
         hs_acc[...] += lane_sum(h)
         return carry
 
-    lax.fori_loop(0, chunks, chunk_step, 0)
+    lax.fori_loop(0, arrivals, chunk_step, 0)
     for copy in w0_copies():
         copy.wait_send()
-    w0_forward().wait_send()
+    for q in range(1, grid_cols):
+        w0_forward(q).wait_send()
     first_wb(row, 0).wait_send()
     first_ws(row, 0).wait_send()
     for half in range(2):
@@ -652,7 +653,7 @@
                 V((2, docs, topics), BF16), V((2, topics, docs), BF16), V((2, EXTRA, topics), F32), V(lanes, F32),
                 V(lanes, F32), partial, exchange, V((rows, DEVICES, EXTRA, topics), F32),
                 V((EXTRA, topics), F32), V((EXTRA, topics), F32),
-                dma((2,)), dma((2,)), dma((2,)), dma, dma((pieces,)), dma((pieces,)), dma((3,)), dma((3,)),
+                dma((2,)), dma((2,)), dma((2,)), dma, dma((mine // ARRIVE,)), dma((mine // ARRIVE,)), dma((cols + 1,)), dma((cols + 1,)),
             ] + [dma((rows, DEVICES))] * 6 + [V((rows, CHIPS, part + EXTRA, topics), F32), dma((rows,)), dma((rows,))] + [dma((pieces,))] * 3 + [dma((2,))] * 2 + [dma((2 * cols,))] * 2,
             compiler_params=pltpu.CompilerParams(vmem_limit_bytes=VMEM, collective_id=0, has_side_effects=True),
             cost_estimate=cost(rows * docs, mine, topics, 18), name="main",

time: 738 us -> 735 us (level)
  no operation moved by 1% of the time
where the time goes in v5:
time: 735 us; the launch traced here: 734 us
  Pallas kernels  727 us (99%)
    pallas_call x1, Pallas kernels, body(): pl.pallas_call(functools.partial(main_kernel, SWEEPS - 3, cols), in_specs...  715 us
  transfers between devices with their start and end apart: 1, of which 1 were waited for; matrix products, arithmetic and copies ran while one was open for 0% of the time, Pallas kernels for 2%

profile of v5, /device:TPU:0, one launch (start us, length us, event | category | flops | bytes accessed | tf_op | source)
XLA Modules:
  0.0 733.9 jit_solution(951826449277866749)
XLA Ops:
  0.6 715.3 %main.1 = (bf16[1024,8192]{1,0:T(8,128)(2,1)}, f32[2,256,8192]{2,1,0:T(8,128)}, f32[256,512]{1,0:T(8,128)}, f32[1024,256]{1,0:T(8,128)}) custom-call(bf16[1024,16384]{1,0:T(8,128)(2,1)} %counts.1, f32[1024,256]{1,0:T(8,128)} %w_in.1, f32[256,16384]{1,0:T(8,128)} %h_in.1), custom_call_target="tpu_custom_call" | custom-call | flops 154618822656 | bytes 33554432 | tf_op jit(solution)/shard_map/main/pallas_call | solution.py:643
  715.9 3.4 collective-permute-start
  719.3 0.0 copy-start
  719.3 11.7 %place.1 = f32[256,16384]{1,0:T(8,128)} custom-call(f32[2,256,8192]{2,1,0:T(8,128)} %get-tuple-element.6.h_pair), custom_call_target="tpu_custom_call" | custom-call | flops 100000000 | bytes 33554432 | tf_op jit(solution)/shard_map/place/pallas_call | solution.py:664
  731.0 1.0 collective-permute-done
  732.1 0.8 constant_dynamic-update-slice_fusion
  732.9 0.0 copy-done
  732.9 1.0 copy.7
Async XLA Ops:
  715.9 16.1 %collective-permute-start = (f32[256,512]{1,0:T(8,128)}, f32[256,512]{1,0:T(8,128)S(1)}, u32[]{:S(2)}, u32[]{:S(2)}) collective-permute-start(f32[256,512]{1,0:T(8,128)} %get-tuple-element.7), channel_id=1, source_target_pairs={{0,4},{4,0},{1,5},{5,1},{2,6},{6,2},{3,7},{7,3}} | collective-permute-start | bytes 1572872 | tf_op jit(solution)/shard_map/ppermute | solution.py:661
  719.3 13.6 %copy-start = (f32[1024,256]{1,0:T(8,128)S(1)}, f32[1024,256]{1,0:T(8,128)}, u32[]{:S(2)}) copy-start(f32[1024,256]{1,0:T(8,128)} %get-tuple-element.10) | copy-start | bytes 3145732

commit v6 on v5

--- a/solution.py
+++ b/solution.py
@@ -597,7 +597,7 @@
 PLACE = 2048
 
 
-def place_kernel(h_pair, h_out, buf, in_sem, out_sem):
+def place_kernel(h_pair, w_in, h_out, w_out, buf, w_buf, in_sem, out_sem):
     row = lax.axis_index("row")
     width = h_pair.shape[2]
     jobs = []
@@ -611,6 +611,8 @@
                 pltpu.make_async_copy(h_pair.at[half, :, pl.ds(start, size)], held, in_sem.at[n]),
                 pltpu.make_async_copy(held, h_out.at[:, pl.ds(pl.multiple_of(half * width + start, PLACE), size)], out_sem.at[n]),
             ))
+    n = len(jobs)
+    jobs.append((pltpu.make_async_copy(w_in, w_buf, in_sem.at[n]), pltpu.make_async_copy(w_buf, w_out, out_sem.at[n])))
     for load, _ in jobs:
         load.start()
     for load, store in jobs:
@@ -661,13 +663,14 @@
         other = lax.ppermute(h_last, "row", [(0, 1), (1, 0)])
         row = lax.axis_index("row")
         jobs = 2 * mine // PLACE
-        h_out = pl.pallas_call(
+        h_out, w_out = pl.pallas_call(
             place_kernel,
-            in_specs=[hbm], out_specs=hbm, out_shape=sds((topics, width), F32),
-            scratch_shapes=[V((jobs, topics, PLACE), F32), dma((jobs,)), dma((jobs,))],
+            in_specs=[hbm, hbm], out_specs=[hbm, hbm],
+            out_shape=[sds((topics, width), F32), sds((docs, topics), F32)],
+            scratch_shapes=[V((jobs, topics, PLACE), F32), V((docs, topics), F32), dma((jobs + 1,)), dma((jobs + 1,))],
             compiler_params=pltpu.CompilerParams(vmem_limit_bytes=VMEM),
             cost_estimate=pl.CostEstimate(flops=10 ** 8, bytes_accessed=8 * topics * width, transcendentals=0), name="place",
-        )(h_pair)
+        )(h_pair, w_out)
         h_out = lax.dynamic_update_slice(h_out, other, (0, (1 - row) * mine + mine - CHUNK))
         return w_out, h_out
 

time: 735 us -> 734 us (level)
  no operation moved by 1% of the time
where the time goes in v6:
time: 734 us; the launch traced here: 733 us
  Pallas kernels  727 us (99%)
    pallas_call x1, Pallas kernels, body(): pl.pallas_call(functools.partial(main_kernel, SWEEPS - 3, cols), in_specs...  715 us
  transfers between devices with their start and end apart: 1, of which 1 were waited for; matrix products, arithmetic and copies ran while one was open for 0% of the time, Pallas kernels for 2%

profile of v6, /device:TPU:0, one launch (start us, length us, event | category | flops | bytes accessed | tf_op | source)
XLA Modules:
  0.0 732.9 jit_solution(13115762476710834024)
XLA Ops:
  0.6 715.3 %main.1 = (bf16[1024,8192]{1,0:T(8,128)(2,1)}, f32[2,256,8192]{2,1,0:T(8,128)}, f32[256,512]{1,0:T(8,128)}, f32[1024,256]{1,0:T(8,128)}) custom-call(bf16[1024,16384]{1,0:T(8,128)(2,1)} %counts.1, f32[1024,256]{1,0:T(8,128)} %w_in.1, f32[256,16384]{1,0:T(8,128)} %h_in.1), custom_call_target="tpu_custom_call" | custom-call | flops 154618822656 | bytes 33554432 | tf_op jit(solution)/shard_map/main/pallas_call | solution.py:645
  715.9 3.4 collective-permute-start
  719.3 12.0 %place.1 = (f32[256,16384]{1,0:T(8,128)}, f32[1024,256]{1,0:T(8,128)}) custom-call(f32[2,256,8192]{2,1,0:T(8,128)} %get-tuple-element.7.h_pair, f32[1024,256]{1,0:T(8,128)} %get-tuple-element.8.w_in), custom_call_target="tpu_custom_call" | custom-call | flops 100000000 | bytes 33554432 | tf_op jit(solution)/shard_map/place/pallas_call | solution.py:666
  731.3 0.8 collective-permute-done
  732.1 0.8 constant_dynamic-update-slice_fusion
Async XLA Ops:
  715.9 16.1 %collective-permute-start = (f32[256,512]{1,0:T(8,128)}, f32[256,512]{1,0:T(8,128)S(1)}, u32[]{:S(2)}, u32[]{:S(2)}) collective-permute-start(f32[256,512]{1,0:T(8,128)} %get-tuple-element.11), channel_id=1, source_target_pairs={{0,4},{4,0},{1,5},{5,1},{2,6},{6,2},{3,7},{7,3}} | collective-permute-start | bytes 1572872 | tf_op jit(solution)/shard_map/ppermute | solution.py:663
